TPU v7x, 1024 devices: a whole 8x8x8 slice. The times are simulated.
1024 devices in a mesh: gx: 8 (over z), gy: 16 (over x, core), gz: 8 (over y).
Axes of the slice: x: 8, y: 8, z: 8, core: 2. Of those that a mesh axis runs over, the one named last changes fastest.
Arguments:
- right_side: float32 [32, 128, 1024], P('gx', 'gy', 'gz'), may hold values from -8 to 8
- diagonal: float32 [32, 128, 1024], P('gx', 'gy', 'gz'), may hold values from 0.2 to 2
- sign_bits: int32 [32, 128, 1024], P('gx', 'gy', 'gz'), may hold values from 0 to 1
- freq_x: int32 [2048], replicated, may hold values from 0 to 31
- freq_y: int32 [2048], replicated, may hold values from 0 to 127
- freq_z: int32 [2048], replicated, may hold values from 0 to 1023
Outputs:
- solution_field: float32 [32, 128, 1024], P('gx', 'gy', 'gz')
- residual: float32 [32, 128, 1024], P('gx', 'gy', 'gz')
All inputs are finite; a program needn't handle non-finite values.
Results may differ from a plain program's by a relative error of at most 0.0009.
Values sent between devices are 32-bit elements; how exact they have to be, the bound alone decides.
No kernel may reach another device: no remote copies, remote signals or barrier semaphores. Data moves between devices by JAX's collectives and lax.ppermute only.
A program may use at most 32 MiB of HBM per device.

v0:
```python
import jax
import jax.numpy as jnp
from jax import lax
from jax.sharding import Mesh
from jax.sharding import PartitionSpec as P

BASIS = 8
ITERS = 2
GY = ("gy_0", "gy_1")
GY_GZ = ("gy_0", "gy_1", "gz")


center_value = 7.0
half_range = 7.0
tiny_value = 1e-06
highest = lax.Precision.HIGHEST


def extended(shard, sides, width):
    for axis, dim in sides:
        size, length = (lax.axis_size(axis), shard.shape[dim])
        up = [(i, (i + 1) % size) for i in range(size - 1)]
        down = [(j, i) for i, j in up]
        last = lax.slice_in_dim(shard, length - width, length, axis=dim)
        first = lax.slice_in_dim(shard, 0, width, axis=dim)
        before = lax.ppermute(last, axis, up)
        after = lax.ppermute(first, axis, down)
        shard = jnp.concatenate([before, shard, after], axis=dim)
    return shard


def padded_2(shard, sides, width):
    edges = {}
    for axis, dim in sides:
        size, length = (lax.axis_size(axis), shard.shape[dim])
        up = [(i, (i + 1) % size) for i in range(size - 1)]
        last = lax.slice_in_dim(shard, length - width, length, axis=dim)
        first = lax.slice_in_dim(shard, 0, width, axis=dim)
        edges[dim] = (
            lax.ppermute(last, axis, up),
            lax.ppermute(first, axis, [(b, a) for a, b in up]),
        )
    done = []
    for _, dim in sides:
        low, high = edges[dim]
        around = [(width, width) if d in done else (0, 0) for d in range(shard.ndim)]
        shard = jnp.concatenate([jnp.pad(low, around), shard, jnp.pad(high, around)], axis=dim)
        done.append(dim)
    return shard


def cut_along(shard, dim, size):
    shape = shard.shape
    tiles = shard.reshape(*shape[:dim], size, shape[dim] // size, *shape[dim + 1 :])
    return jnp.moveaxis(tiles, dim, 0)


def sent_and_summed(shard, axis, dim):
    tiles = cut_along(shard, dim, lax.axis_size(axis))
    arrived = lax.all_to_all(tiles, axis, split_axis=0, concat_axis=0, tiled=True)
    return arrived.sum(axis=0)


def one_axis_at_a_time(shard, axes):
    for axis in axes:
        shard = lax.psum(shard, axis)
    return shard


def from_everyone(shard, axis):
    size = lax.axis_size(axis)
    return lax.all_to_all(
        jnp.broadcast_to(shard[None], (size, *shard.shape)), axis, 0, 0, tiled=True
    )


def laid_out(tiles, dim):
    shape = list(tiles.shape[1:])
    shape[dim] *= tiles.shape[0]
    return jnp.moveaxis(tiles, 0, dim).reshape(shape)


def gather_directly(shard, axis, dim):
    tiles = from_everyone(shard, axis)
    return laid_out(tiles, dim)


def stencil(padded, diagonal):
    beside = padded[2:, 1:-1, 1:-1] + padded[:-2, 1:-1, 1:-1]
    beside = beside + padded[1:-1, 2:, 1:-1] + padded[1:-1, :-2, 1:-1]
    beside = beside + padded[1:-1, 1:-1, 2:] + padded[1:-1, 1:-1, :-2]
    return (6.0 + diagonal) * padded[1:-1, 1:-1, 1:-1] - beside


def cosine_table(freqs, offset, count, length):
    indices = offset + jnp.arange(count, dtype=jnp.int32)
    phases = (2 * indices[:, None] + 1) * freqs[None, :] % (4 * length)
    return (jnp.sqrt(2.0 / length) * jnp.cos(jnp.pi * phases / (2.0 * length))).astype(jnp.float32)


def least_squares(matrix):
    count = matrix.shape[0] - 1
    target = matrix[count]
    orthonormal = []
    upper = {}
    for column_at in range(count):
        column = matrix[column_at]
        for repeat in range(2):
            for earlier in range(column_at):
                amount = jnp.dot(orthonormal[earlier], column, precision=highest)
                column = column - amount * orthonormal[earlier]
                upper[earlier, column_at] = upper.get((earlier, column_at), 0.0) + amount
        length = jnp.sqrt(jnp.dot(column, column, precision=highest) + tiny_value)
        orthonormal.append(column / length)
        upper[column_at, column_at] = length
    projected = [jnp.dot(basis_row, target, precision=highest) for basis_row in orthonormal]
    solved = [None] * count
    for row_at in range(count - 1, -1, -1):
        value = projected[row_at]
        for later in range(row_at + 1, count):
            value = value - upper[row_at, later] * solved[later]
        solved[row_at] = value / upper[row_at, row_at]
    return jnp.stack(solved)


def grid_mask(size_x, size_y, size_z):
    along_x = lax.axis_index("gx") * size_x + jnp.arange(size_x + 2, dtype=jnp.int32) - 1
    along_y = lax.axis_index(GY) * size_y + jnp.arange(size_y + 2, dtype=jnp.int32) - 1
    along_z = lax.axis_index("gz") * size_z + jnp.arange(size_z + 2, dtype=jnp.int32) - 1
    keep_x = (along_x >= 0) & (along_x < size_x * lax.axis_size("gx"))
    keep_y = (along_y >= 0) & (along_y < size_y * lax.axis_size(GY))
    keep_z = (along_z >= 0) & (along_z < size_z * lax.axis_size("gz"))
    return keep_x[:, None, None] & keep_y[None, :, None] & keep_z[None, None, :]


def basis_deep(residual, diagonal, rimmed, inside):
    vectors = [residual]
    images = []
    for position in range(0, BASIS, 2):
        previous = vectors[position - 1] if position > 0 else jnp.zeros_like(residual)
        widened, widened_prev = (
            extended(vectors[position], (("gx", 0), (GY, 1), ("gz", 2)), 2),
            extended(previous, (("gx", 0), (GY, 1), ("gz", 2)), 2),
        )
        image_rim = stencil(widened, rimmed)
        images.append(image_rim[1:-1, 1:-1, 1:-1])
        turned = (image_rim - center_value * widened[1:-1, 1:-1, 1:-1]) / half_range
        following = turned if position == 0 else 2.0 * turned - widened_prev[1:-1, 1:-1, 1:-1]
        following = jnp.where(inside, following, 0.0)
        vectors.append(following[1:-1, 1:-1, 1:-1])
        image = stencil(following, diagonal)
        images.append(image)
        if position + 2 < BASIS:
            turned = (image - center_value * vectors[position + 1]) / half_range
            vectors.append(2.0 * turned - vectors[position])
    return (vectors, images)


def local_sketch(columns, signs, table_x, table_y, table_z):
    flipped = jnp.stack(columns, axis=2) * signs[:, :, None, :]
    size_x, size_y, count, depth = flipped.shape
    rows_flat = flipped.reshape(-1, depth)
    weights = table_x[:, None, :] * table_y[None, :, :]
    sampled = table_z.shape[1]
    block = min(512, sampled)
    pieces = []
    for begin in range(0, sampled, block):
        inner_sums = jnp.dot(
            rows_flat,
            table_z[:, begin : begin + block],
            precision=highest,
            preferred_element_type=jnp.float32,
        )
        inner_sums = inner_sums.reshape(size_x, size_y, count, block)
        pieces.append(
            jnp.einsum(
                "xyjs,xys->js", inner_sums, weights[:, :, begin : begin + block], precision=highest
            )
        )
    return jnp.concatenate(pieces, axis=1)


def shards(right_side, diagonal, sign_bits, freq_x, freq_y, freq_z):
    size_x, size_y, size_z = right_side.shape
    table_x = cosine_table(
        freq_x, lax.axis_index("gx") * size_x, size_x, size_x * lax.axis_size("gx")
    )
    table_y = cosine_table(freq_y, lax.axis_index(GY) * size_y, size_y, size_y * lax.axis_size(GY))
    table_z = cosine_table(
        freq_z, lax.axis_index("gz") * size_z, size_z, size_z * lax.axis_size("gz")
    )
    signs = 1.0 - 2.0 * sign_bits.astype(jnp.float32)
    rimmed = padded_2(diagonal, (("gx", 0), (GY, 1), ("gz", 2)), 1)
    inside = grid_mask(size_x, size_y, size_z)
    solution = jnp.zeros_like(right_side)
    residual = right_side
    for restart in range(ITERS):
        vectors, images = basis_deep(residual, diagonal, rimmed, inside)
        partial_value = local_sketch(images + [residual], signs, table_x, table_y, table_z)
        shares = sent_and_summed(partial_value, "gx", 1)
        shares = one_axis_at_a_time(shares, GY_GZ)
        matrix = gather_directly(shares, "gx", 1)
        weights_solved = least_squares(matrix)
        for position in range(BASIS):
            solution = solution + weights_solved[position] * vectors[position]
            residual = residual - weights_solved[position] * images[position]
    return (solution, residual)


def solution(mesh):
    split = Mesh(
        mesh.devices.reshape(mesh.shape["gx"], 8, 2, mesh.shape["gz"]), ("gx", "gy_0", "gy_1", "gz")
    )
    return jax.shard_map(
        shards,
        mesh=split,
        in_specs=(P("gx", GY, "gz"), P("gx", GY, "gz"), P("gx", GY, "gz"), P(), P(), P()),
        out_specs=(P("gx", GY, "gz"), P("gx", GY, "gz")),
        check_vma=False,
    )
```

profile of v0, /device:TPU:1, one launch (start us, length us, event | category | flops | bytes accessed | tf_op | source)
XLA Modules:
  0.0 758.2 jit_solution(1742615286080373125)
XLA Ops:
  1.4 4.5 collective-permute-start.1
  5.9 12.8 %collective-permute-start.4 = (f32[4,1,128]{2,1,0:T(1,128)S(1)}, f32[4,1,128]{2,1,0:T(1,128)S(1)}, u32[]{:S(2)}, u32[]{:S(2)}) collective-permute-start(f32[4,1,128]{2,1,0:T(1,128)S(1)} %get-tuple-element.253), channel_id=1, source_target_pairs={{8,0},{16,8},{24,16},{32,24},{40,32},{48,40},{56,48},{64,56},{72,6... | collective-permute-start | bytes 6152 | tf_op jit(solution)/shard_map/ppermute | solution.py:41
  53.0 5.1 collective-permute-start.12
  59.5 6.7 collective-permute-start.18
  67.5 4.3 collective-permute-start.14
  85.1 4.4 collective-permute-start.22
  91.0 4.9 collective-permute-done.23
  96.5 4.6 collective-permute-start.24
  102.5 5.5 collective-permute-start.30
  109.3 5.6 collective-permute-start.26
  127.7 4.3 collective-permute-start.34
  133.5 5.0 collective-permute-done.35
  139.1 5.5 collective-permute-start.36
  146.0 5.5 collective-permute-start.42
  152.8 5.6 collective-permute-start.38
  171.2 4.3 collective-permute-start.46
  185.9 22.2 %all_to_all.20 = f32[8,9,256]{2,1,0:T(8,128)S(1)} all-to-all(f32[8,9,256]{2,1,0:T(8,128)S(1)} %copy.12), channel_id=1, replica_groups=mesh['gx'=8,'gy_0'=8,'gy_1'=2,'gz'=8] {'gx'}, dimensions={0} | all-to-all | bytes 147456 | tf_op jit(solution)/shard_map/all_to_all | solution.py:60
  208.2 30.7 %psum.42 = f32[9,256]{1,0:T(8,128)S(1)} all-reduce(f32[9,256]{1,0:T(8,128)S(1)} %reduce_sum.18), channel_id=1, replica_groups=mesh['gx'=8,'gy_0'=8,'gy_1'=2,'gz'=8] {'gy_0'}, use_global_device_ids=true, to_apply=%region_1.2 | all-reduce | flops 2304 | bytes 18432 | tf_op jit(solution)/shard_map/psum | solution.py:66
  238.9 11.7 %psum.43 = f32[9,256]{1,0:T(8,128)S(1)} all-reduce(f32[9,256]{1,0:T(8,128)S(1)} %psum.42), channel_id=1, replica_groups=mesh['gx'=8,'gy_0'=8,'gy_1'=2,'gz'=8] {'gy_1'}, use_global_device_ids=true, to_apply=%region_2.3 | all-reduce | flops 2304 | bytes 18432 | tf_op jit(solution)/shard_map/psum | solution.py:66
  250.6 23.5 %psum.44 = f32[9,256]{1,0:T(8,128)S(1)} all-reduce(f32[9,256]{1,0:T(8,128)S(1)} %psum.43), channel_id=1, replica_groups=mesh['gx'=8,'gy_0'=8,'gy_1'=2,'gz'=8] {'gz'}, use_global_device_ids=true, to_apply=%region_3.4 | all-reduce | flops 2304 | bytes 18432 | tf_op jit(solution)/shard_map/psum | solution.py:66
  274.1 10.3 %all_to_all.21 = f32[8,9,256]{2,1,0:T(8,128)S(1)} all-to-all(f32[8,9,256]{2,1,0:T(8,128)S(1)} %broadcast_in_dim.16), channel_id=1, replica_groups=mesh['gx'=8,'gy_0'=8,'gy_1'=2,'gz'=8] {'gx'}, dimensions={0} | all-to-all | bytes 147456 | tf_op jit(solution)/shard_map/all_to_all | solution.py:72
  402.5 12.8 %collective-permute-start.50 = (f32[8,2,128]{2,1,0:T(2,128)S(1)}, f32[8,2,128]{2,1,0:T(2,128)S(1)}, u32[]{:S(2)}, u32[]{:S(2)}) collective-permute-start(f32[8,2,128]{2,1,0:T(2,128)S(1)} %get-tuple-element.220), channel_id=1, source_target_pairs={{0,8},{8,16},{16,24},{24,32},{32,40},{40,48},{48,56},{56,64},{64,7... | collective-permute-start | bytes 24584 | tf_op jit(solution)/shard_map/ppermute | solution.py:26
  453.4 4.7 collective-permute-start.64
  459.6 5.0 collective-permute-done.65
  476.3 5.9 collective-permute-start.68
  494.9 4.3 collective-permute-start.76
  516.8 5.9 collective-permute-start.80
  550.2 21.2 %all_to_all.22 = f32[8,9,256]{2,1,0:T(8,128)S(1)} all-to-all(f32[8,9,256]{2,1,0:T(8,128)S(1)} %copy.17), channel_id=1, replica_groups=mesh['gx'=8,'gy_0'=8,'gy_1'=2,'gz'=8] {'gx'}, dimensions={0} | all-to-all | bytes 147456 | tf_op jit(solution)/shard_map/all_to_all | solution.py:60
  571.4 28.4 %psum.45 = f32[9,256]{1,0:T(8,128)S(1)} all-reduce(f32[9,256]{1,0:T(8,128)S(1)} %reduce_sum.19), channel_id=1, replica_groups=mesh['gx'=8,'gy_0'=8,'gy_1'=2,'gz'=8] {'gy_0'}, use_global_device_ids=true, to_apply=%region_5.6 | all-reduce | flops 2304 | bytes 18432 | tf_op jit(solution)/shard_map/psum | solution.py:66
  599.9 11.7 %psum.46 = f32[9,256]{1,0:T(8,128)S(1)} all-reduce(f32[9,256]{1,0:T(8,128)S(1)} %psum.45), channel_id=1, replica_groups=mesh['gx'=8,'gy_0'=8,'gy_1'=2,'gz'=8] {'gy_1'}, use_global_device_ids=true, to_apply=%region_6.7 | all-reduce | flops 2304 | bytes 18432 | tf_op jit(solution)/shard_map/psum | solution.py:66
  611.6 23.5 %psum.47 = f32[9,256]{1,0:T(8,128)S(1)} all-reduce(f32[9,256]{1,0:T(8,128)S(1)} %psum.46), channel_id=1, replica_groups=mesh['gx'=8,'gy_0'=8,'gy_1'=2,'gz'=8] {'gz'}, use_global_device_ids=true, to_apply=%region_7.8 | all-reduce | flops 2304 | bytes 18432 | tf_op jit(solution)/shard_map/psum | solution.py:66
  635.1 10.3 %all_to_all.23 = f32[8,9,256]{2,1,0:T(8,128)S(1)} all-to-all(f32[8,9,256]{2,1,0:T(8,128)S(1)} %broadcast_in_dim.17), channel_id=1, replica_groups=mesh['gx'=8,'gy_0'=8,'gy_1'=2,'gz'=8] {'gx'}, dimensions={0} | all-to-all | bytes 147456 | tf_op jit(solution)/shard_map/all_to_all | solution.py:72
  (486 shorter events, 340.5 us)
Async XLA Ops:
  1.4 51.0 %collective-permute-start.1 = (f32[4,1,128]{2,1,0:T(1,128)S(1)}, f32[4,1,128]{2,1,0:T(1,128)S(1)}, u32[]{:S(2)}, u32[]{:S(2)}) collective-permute-start(f32[4,1,128]{2,1,0:T(1,128)S(1)} %get-tuple-element.252), channel_id=1, source_target_pairs={{0,8},{8,16},{16,24},{24,32},{32,40},{40,48},{48,56},{56,64},{64,7... | collective-permute-start | bytes 6152 | tf_op jit(solution)/shard_map/ppermute | solution.py:40
  5.9 46.5 %collective-permute-start.4 = (f32[4,1,128]{2,1,0:T(1,128)S(1)}, f32[4,1,128]{2,1,0:T(1,128)S(1)}, u32[]{:S(2)}, u32[]{:S(2)}) collective-permute-start(f32[4,1,128]{2,1,0:T(1,128)S(1)} %get-tuple-element.253), channel_id=1, source_target_pairs={{8,0},{16,8},{24,16},{32,24},{40,32},{48,40},{56,48},{64,56},{72,6... | collective-permute-start | bytes 6152 | tf_op jit(solution)/shard_map/ppermute | solution.py:41
  19.5 14.5 %collective-permute-start.7 = (f32[2,8,128]{2,1,0:T(8,128)S(1)}, f32[2,8,128]{2,1,0:T(8,128)S(1)}, u32[]{:S(2)}, u32[]{:S(2)}) collective-permute-start(f32[2,8,128]{2,1,0:T(8,128)S(1)} %get-tuple-element.256), channel_id=1, source_target_pairs={{128,0},{256,128},{384,256},{512,384},{640,512},{768,640},{896,768... | collective-permute-start | bytes 24584 | tf_op jit(solution)/shard_map/ppermute | solution.py:27
  20.8 12.5 %collective-permute-start.6 = (f32[2,8,128]{2,1,0:T(8,128)S(1)}, f32[2,8,128]{2,1,0:T(8,128)S(1)}, u32[]{:S(2)}, u32[]{:S(2)}) collective-permute-start(f32[2,8,128]{2,1,0:T(8,128)S(1)} %get-tuple-element.257), channel_id=1, source_target_pairs={{0,128},{128,256},{256,384},{384,512},{512,640},{640,768},{768,896... | collective-permute-start | bytes 24584 | tf_op jit(solution)/shard_map/ppermute | solution.py:26
  24.8 18.7 %collective-permute-start = (f32[4,8,1]{2,1,0:T(8,128)S(1)}, f32[4,8,1]{2,1,0:T(8,128)S(1)}, u32[]{:S(2)}, u32[]{:S(2)}) collective-permute-start(f32[4,8,1]{2,1,0:T(8,128)S(1)} %get-tuple-element.250), channel_id=1, source_target_pairs={{0,1},{1,2},{2,3},{3,4},{4,5},{5,6},{6,7},{8,9},{9,10},{10,11},{11... | collective-permute-start | bytes 392 | tf_op jit(solution)/shard_map/ppermute | solution.py:40
  53.0 14.5 %collective-permute-start.12 = (f32[2,8,128]{2,1,0:T(8,128)S(1)}, f32[2,8,128]{2,1,0:T(8,128)S(1)}, u32[]{:S(2)}, u32[]{:S(2)}) collective-permute-start(f32[2,8,128]{2,1,0:T(8,128)S(1)} %get-tuple-element.248), channel_id=1, source_target_pairs={{0,128},{128,256},{256,384},{384,512},{512,640},{640,768},{768,896... | collective-permute-start | bytes 24584 | tf_op jit(solution)/shard_map/ppermute | solution.py:26
  59.5 14.3 %collective-permute-start.18 = (f32[2,8,128]{2,1,0:T(8,128)S(1)}, f32[2,8,128]{2,1,0:T(8,128)S(1)}, u32[]{:S(2)}, u32[]{:S(2)}) collective-permute-start(f32[2,8,128]{2,1,0:T(8,128)S(1)} %get-tuple-element.178), channel_id=1, source_target_pairs={{0,128},{128,256},{256,384},{384,512},{512,640},{640,768},{768,896... | collective-permute-start | bytes 24584 | tf_op jit(solution)/shard_map/ppermute | solution.py:26
  67.5 11.9 %collective-permute-start.14 = (f32[8,2,128]{2,1,0:T(2,128)S(1)}, f32[8,2,128]{2,1,0:T(2,128)S(1)}, u32[]{:S(2)}, u32[]{:S(2)}) collective-permute-start(f32[8,2,128]{2,1,0:T(2,128)S(1)} %get-tuple-element.230), channel_id=1, source_target_pairs={{0,8},{8,16},{16,24},{24,32},{32,40},{40,48},{48,56},{56,64},{64,7... | collective-permute-start | bytes 24584 | tf_op jit(solution)/shard_map/ppermute | solution.py:26
  73.8 11.1 %collective-permute-start.20 = (f32[8,2,128]{2,1,0:T(2,128)S(1)}, f32[8,2,128]{2,1,0:T(2,128)S(1)}, u32[]{:S(2)}, u32[]{:S(2)}) collective-permute-start(f32[8,2,128]{2,1,0:T(2,128)S(1)} %get-tuple-element.232), channel_id=1, source_target_pairs={{0,8},{8,16},{16,24},{24,32},{32,40},{40,48},{48,56},{56,64},{64,7... | collective-permute-start | bytes 24584 | tf_op jit(solution)/shard_map/ppermute | solution.py:26
  79.6 11.2 %collective-permute-start.16 = (f32[8,12,2]{2,1,0:T(8,128)S(1)}, f32[8,12,2]{2,1,0:T(8,128)S(1)}, u32[]{:S(2)}, u32[]{:S(2)}) collective-permute-start(f32[8,12,2]{2,1,0:T(8,128)S(1)} %get-tuple-element.202), channel_id=1, source_target_pairs={{0,1},{1,2},{2,3},{3,4},{4,5},{5,6},{6,7},{8,9},{9,10},{10,11},{11... | collective-permute-start | bytes 2312 | tf_op jit(solution)/shard_map/ppermute | solution.py:26
  96.5 12.8 %collective-permute-start.24 = (f32[2,8,128]{2,1,0:T(8,128)S(1)}, f32[2,8,128]{2,1,0:T(8,128)S(1)}, u32[]{:S(2)}, u32[]{:S(2)}) collective-permute-start(f32[2,8,128]{2,1,0:T(8,128)S(1)} %get-tuple-element.246), channel_id=1, source_target_pairs={{0,128},{128,256},{256,384},{384,512},{512,640},{640,768},{768,896... | collective-permute-start | bytes 24584 | tf_op jit(solution)/shard_map/ppermute | solution.py:26
  102.5 14.4 %collective-permute-start.30 = (f32[2,8,128]{2,1,0:T(8,128)S(1)}, f32[2,8,128]{2,1,0:T(8,128)S(1)}, u32[]{:S(2)}, u32[]{:S(2)}) collective-permute-start(f32[2,8,128]{2,1,0:T(8,128)S(1)} %get-tuple-element.174), channel_id=1, source_target_pairs={{0,128},{128,256},{256,384},{384,512},{512,640},{640,768},{768,896... | collective-permute-start | bytes 24584 | tf_op jit(solution)/shard_map/ppermute | solution.py:26
  109.3 13.2 %collective-permute-start.26 = (f32[8,2,128]{2,1,0:T(2,128)S(1)}, f32[8,2,128]{2,1,0:T(2,128)S(1)}, u32[]{:S(2)}, u32[]{:S(2)}) collective-permute-start(f32[8,2,128]{2,1,0:T(2,128)S(1)} %get-tuple-element.226), channel_id=1, source_target_pairs={{0,8},{8,16},{16,24},{24,32},{32,40},{40,48},{48,56},{56,64},{64,7... | collective-permute-start | bytes 24584 | tf_op jit(solution)/shard_map/ppermute | solution.py:26
  116.9 10.7 %collective-permute-start.32 = (f32[8,2,128]{2,1,0:T(2,128)S(1)}, f32[8,2,128]{2,1,0:T(2,128)S(1)}, u32[]{:S(2)}, u32[]{:S(2)}) collective-permute-start(f32[8,2,128]{2,1,0:T(2,128)S(1)} %get-tuple-element.228), channel_id=1, source_target_pairs={{0,8},{8,16},{16,24},{24,32},{32,40},{40,48},{48,56},{56,64},{64,7... | collective-permute-start | bytes 24584 | tf_op jit(solution)/shard_map/ppermute | solution.py:26
  139.1 13.6 %collective-permute-start.36 = (f32[2,8,128]{2,1,0:T(8,128)S(1)}, f32[2,8,128]{2,1,0:T(8,128)S(1)}, u32[]{:S(2)}, u32[]{:S(2)}) collective-permute-start(f32[2,8,128]{2,1,0:T(8,128)S(1)} %get-tuple-element.244), channel_id=1, source_target_pairs={{0,128},{128,256},{256,384},{384,512},{512,640},{640,768},{768,896... | collective-permute-start | bytes 24584 | tf_op jit(solution)/shard_map/ppermute | solution.py:26
  146.0 14.4 %collective-permute-start.42 = (f32[2,8,128]{2,1,0:T(8,128)S(1)}, f32[2,8,128]{2,1,0:T(8,128)S(1)}, u32[]{:S(2)}, u32[]{:S(2)}) collective-permute-start(f32[2,8,128]{2,1,0:T(8,128)S(1)} %get-tuple-element.170), channel_id=1, source_target_pairs={{0,128},{128,256},{256,384},{384,512},{512,640},{640,768},{768,896... | collective-permute-start | bytes 24584 | tf_op jit(solution)/shard_map/ppermute | solution.py:26
  152.8 13.2 %collective-permute-start.38 = (f32[8,2,128]{2,1,0:T(2,128)S(1)}, f32[8,2,128]{2,1,0:T(2,128)S(1)}, u32[]{:S(2)}, u32[]{:S(2)}) collective-permute-start(f32[8,2,128]{2,1,0:T(2,128)S(1)} %get-tuple-element.222), channel_id=1, source_target_pairs={{0,8},{8,16},{16,24},{24,32},{32,40},{40,48},{48,56},{56,64},{64,7... | collective-permute-start | bytes 24584 | tf_op jit(solution)/shard_map/ppermute | solution.py:26
  160.4 10.7 %collective-permute-start.44 = (f32[8,2,128]{2,1,0:T(2,128)S(1)}, f32[8,2,128]{2,1,0:T(2,128)S(1)}, u32[]{:S(2)}, u32[]{:S(2)}) collective-permute-start(f32[8,2,128]{2,1,0:T(2,128)S(1)} %get-tuple-element.224), channel_id=1, source_target_pairs={{0,8},{8,16},{16,24},{24,32},{32,40},{40,48},{48,56},{56,64},{64,7... | collective-permute-start | bytes 24584 | tf_op jit(solution)/shard_map/ppermute | solution.py:26
  166.1 10.8 %collective-permute-start.40 = (f32[8,12,2]{2,1,0:T(8,128)S(1)}, f32[8,12,2]{2,1,0:T(8,128)S(1)}, u32[]{:S(2)}, u32[]{:S(2)}) collective-permute-start(f32[8,12,2]{2,1,0:T(8,128)S(1)} %get-tuple-element.194), channel_id=1, source_target_pairs={{0,1},{1,2},{2,3},{3,4},{4,5},{5,6},{6,7},{8,9},{9,10},{10,11},{11... | collective-permute-start | bytes 2312 | tf_op jit(solution)/shard_map/ppermute | solution.py:26
  402.5 14.7 %collective-permute-start.50 = (f32[8,2,128]{2,1,0:T(2,128)S(1)}, f32[8,2,128]{2,1,0:T(2,128)S(1)}, u32[]{:S(2)}, u32[]{:S(2)}) collective-permute-start(f32[8,2,128]{2,1,0:T(2,128)S(1)} %get-tuple-element.220), channel_id=1, source_target_pairs={{0,8},{8,16},{16,24},{24,32},{32,40},{40,48},{48,56},{56,64},{64,7... | collective-permute-start | bytes 24584 | tf_op jit(solution)/shard_map/ppermute | solution.py:26
  431.4 11.2 %collective-permute-start.60 = (f32[2,8,128]{2,1,0:T(8,128)S(1)}, f32[2,8,128]{2,1,0:T(8,128)S(1)}, u32[]{:S(2)}, u32[]{:S(2)}) collective-permute-start(f32[2,8,128]{2,1,0:T(8,128)S(1)} %get-tuple-element.164), channel_id=1, source_target_pairs={{0,128},{128,256},{256,384},{384,512},{512,640},{640,768},{768,896... | collective-permute-start | bytes 24584 | tf_op jit(solution)/shard_map/ppermute | solution.py:26
  436.8 11.5 %collective-permute-start.56 = (f32[8,2,128]{2,1,0:T(2,128)S(1)}, f32[8,2,128]{2,1,0:T(2,128)S(1)}, u32[]{:S(2)}, u32[]{:S(2)}) collective-permute-start(f32[8,2,128]{2,1,0:T(2,128)S(1)} %get-tuple-element.216), channel_id=1, source_target_pairs={{0,8},{8,16},{16,24},{24,32},{32,40},{40,48},{48,56},{56,64},{64,7... | collective-permute-start | bytes 24584 | tf_op jit(solution)/shard_map/ppermute | solution.py:26
  442.7 10.7 %collective-permute-start.62 = (f32[8,2,128]{2,1,0:T(2,128)S(1)}, f32[8,2,128]{2,1,0:T(2,128)S(1)}, u32[]{:S(2)}, u32[]{:S(2)}) collective-permute-start(f32[8,2,128]{2,1,0:T(2,128)S(1)} %get-tuple-element.218), channel_id=1, source_target_pairs={{0,8},{8,16},{16,24},{24,32},{32,40},{40,48},{48,56},{56,64},{64,7... | collective-permute-start | bytes 24584 | tf_op jit(solution)/shard_map/ppermute | solution.py:26
  448.4 11.1 %collective-permute-start.58 = (f32[8,12,2]{2,1,0:T(8,128)S(1)}, f32[8,12,2]{2,1,0:T(8,128)S(1)}, u32[]{:S(2)}, u32[]{:S(2)}) collective-permute-start(f32[8,12,2]{2,1,0:T(8,128)S(1)} %get-tuple-element.188), channel_id=1, source_target_pairs={{0,1},{1,2},{2,3},{3,4},{4,5},{5,6},{6,7},{8,9},{9,10},{10,11},{11... | collective-permute-start | bytes 2312 | tf_op jit(solution)/shard_map/ppermute | solution.py:26
  465.3 10.9 %collective-permute-start.66 = (f32[2,8,128]{2,1,0:T(8,128)S(1)}, f32[2,8,128]{2,1,0:T(8,128)S(1)}, u32[]{:S(2)}, u32[]{:S(2)}) collective-permute-start(f32[2,8,128]{2,1,0:T(8,128)S(1)} %get-tuple-element.238), channel_id=1, source_target_pairs={{0,128},{128,256},{256,384},{384,512},{512,640},{640,768},{768,896... | collective-permute-start | bytes 24584 | tf_op jit(solution)/shard_map/ppermute | solution.py:26
  471.0 13.2 %collective-permute-start.72 = (f32[2,8,128]{2,1,0:T(8,128)S(1)}, f32[2,8,128]{2,1,0:T(8,128)S(1)}, u32[]{:S(2)}, u32[]{:S(2)}) collective-permute-start(f32[2,8,128]{2,1,0:T(8,128)S(1)} %get-tuple-element.160), channel_id=1, source_target_pairs={{0,128},{128,256},{256,384},{384,512},{512,640},{640,768},{768,896... | collective-permute-start | bytes 24584 | tf_op jit(solution)/shard_map/ppermute | solution.py:26
  476.3 13.5 %collective-permute-start.68 = (f32[8,2,128]{2,1,0:T(2,128)S(1)}, f32[8,2,128]{2,1,0:T(2,128)S(1)}, u32[]{:S(2)}, u32[]{:S(2)}) collective-permute-start(f32[8,2,128]{2,1,0:T(2,128)S(1)} %get-tuple-element.212), channel_id=1, source_target_pairs={{0,8},{8,16},{16,24},{24,32},{32,40},{40,48},{48,56},{56,64},{64,7... | collective-permute-start | bytes 24584 | tf_op jit(solution)/shard_map/ppermute | solution.py:26
  484.2 10.7 %collective-permute-start.74 = (f32[8,2,128]{2,1,0:T(2,128)S(1)}, f32[8,2,128]{2,1,0:T(2,128)S(1)}, u32[]{:S(2)}, u32[]{:S(2)}) collective-permute-start(f32[8,2,128]{2,1,0:T(2,128)S(1)} %get-tuple-element.214), channel_id=1, source_target_pairs={{0,8},{8,16},{16,24},{24,32},{32,40},{40,48},{48,56},{56,64},{64,7... | collective-permute-start | bytes 24584 | tf_op jit(solution)/shard_map/ppermute | solution.py:26
  505.6 11.2 %collective-permute-start.78 = (f32[2,8,128]{2,1,0:T(8,128)S(1)}, f32[2,8,128]{2,1,0:T(8,128)S(1)}, u32[]{:S(2)}, u32[]{:S(2)}) collective-permute-start(f32[2,8,128]{2,1,0:T(8,128)S(1)} %get-tuple-element.236), channel_id=1, source_target_pairs={{0,128},{128,256},{256,384},{384,512},{512,640},{640,768},{768,896... | collective-permute-start | bytes 24584 | tf_op jit(solution)/shard_map/ppermute | solution.py:26
  511.4 13.2 %collective-permute-start.84 = (f32[2,8,128]{2,1,0:T(8,128)S(1)}, f32[2,8,128]{2,1,0:T(8,128)S(1)}, u32[]{:S(2)}, u32[]{:S(2)}) collective-permute-start(f32[2,8,128]{2,1,0:T(8,128)S(1)} %get-tuple-element.158), channel_id=1, source_target_pairs={{0,128},{128,256},{256,384},{384,512},{512,640},{640,768},{768,896... | collective-permute-start | bytes 24584 | tf_op jit(solution)/shard_map/ppermute | solution.py:26
  516.8 13.5 %collective-permute-start.80 = (f32[8,2,128]{2,1,0:T(2,128)S(1)}, f32[8,2,128]{2,1,0:T(2,128)S(1)}, u32[]{:S(2)}, u32[]{:S(2)}) collective-permute-start(f32[8,2,128]{2,1,0:T(2,128)S(1)} %get-tuple-element.208), channel_id=1, source_target_pairs={{0,8},{8,16},{16,24},{24,32},{32,40},{40,48},{48,56},{56,64},{64,7... | collective-permute-start | bytes 24584 | tf_op jit(solution)/shard_map/ppermute | solution.py:26
  524.7 10.7 %collective-permute-start.86 = (f32[8,2,128]{2,1,0:T(2,128)S(1)}, f32[8,2,128]{2,1,0:T(2,128)S(1)}, u32[]{:S(2)}, u32[]{:S(2)}) collective-permute-start(f32[8,2,128]{2,1,0:T(2,128)S(1)} %get-tuple-element.210), channel_id=1, source_target_pairs={{0,8},{8,16},{16,24},{24,32},{32,40},{40,48},{48,56},{56,64},{64,7... | collective-permute-start | bytes 24584 | tf_op jit(solution)/shard_map/ppermute | solution.py:26
  (64 other events, 423.4 us)
where the time goes:
time: 771 us; the launch traced here: 758 us
  starting transfers between devices  267 us (35%)
  blocking collectives  194 us (25%)
  other arithmetic  140 us (18%)
  between operations  96.9 us (13%)
  waiting for transfers between devices  44.6 us (6%)
  matrix products  8 us (1%)
    ppermute x42, starting transfers between devices, extended(): before = lax.ppermute(last, axis, up)  180 us
    psum x6, blocking collectives, one_axis_at_a_time(): shard = lax.psum(shard, axis)  130 us
    sub x70, other arithmetic, least_squares(): column = column - amount * orthonormal[earlier]  71.8 us
    ppermute x42, starting transfers between devices, extended(): after = lax.ppermute(first, axis, down)  63.9 us
    dot_general x68, other arithmetic, least_squares(): amount = jnp.dot(orthonormal[earlier], column, precision=highest)  44.1 us
    all_to_all x2, blocking collectives, sent_and_summed(): lax.all_to_all(tiles, axis, split_axis=0, concat_axis=0, tiled=True)  43.5 us
    ppermute x42, waiting for transfers between devices, extended(): after = lax.ppermute(first, axis, down)  40.7 us
    all_to_all x2, blocking collectives, from_everyone(): lax.all_to_all(jnp.broadcast_to(shard[None], (size, *shard.shape)), axis,...  20.6 us
  transfers between devices with their start and end apart: 90, of which 12 were waited for; matrix products, arithmetic and copies ran while one was open for 1% of the time, Pallas kernels for 0%

commit v1 on v0

v1 whole, which is shorter than its diff:
```python
import jax
import jax.numpy as jnp
from jax import lax
from jax.experimental import pallas as pl
from jax.experimental.pallas import tpu as pltpu
from jax.sharding import Mesh
from jax.sharding import PartitionSpec as P

BASIS = 8
DEGREE = 2 * BASIS
NX, NY, NZ, SKETCH = 32, 128, 1024, 2048
GX, GZ = 8, 8
SHARE = SKETCH // GX
GY = ("gy_0", "gy_1")
tiny_value = 1e-06
VMEM = pltpu.VMEM
f32, bf16 = jnp.float32, jnp.bfloat16


def shifted(value, axis_name, size, by):
    pairs = [(i, i + by) for i in range(size) if 0 <= i + by < size]
    return lax.ppermute(value, axis_name, pairs)


def cosine_table(freqs, offset, count, length):
    indices = offset + jnp.arange(count, dtype=jnp.int32)
    phases = (2 * indices[:, None] + 1) * freqs[None, :] % (4 * length)
    return (jnp.sqrt(2.0 / length) * jnp.cos(jnp.pi * phases / (2.0 * length))).astype(f32)


def split_3(value):
    high = value.astype(bf16)
    rest = value - high.astype(f32)
    middle = rest.astype(bf16)
    low = (rest - middle.astype(f32)).astype(bf16)
    return high, middle, low


def around(field, value):
    rows, lanes = value.shape
    beside = pltpu.roll(value, 1, 0) + pltpu.roll(value, rows - 1, 0)
    return field + beside + (pltpu.roll(value, 1, 1) + pltpu.roll(value, lanes - 1, 1))


def basis_kernel(at_ref, mid_ref, ym2_ref, ym1_ref, yp1_ref, yp2_ref, t1_ref, t2_ref, t3_ref, w_ref,
                 part_ref, kept_ref, ka_ref, kb_ref, even, odd, coef, lhs):
    gx, gy, gz = at_ref[0], at_ref[1], at_ref[2]
    row = lax.broadcasted_iota(jnp.int32, (40, 256), 0) - 16 + gy * 8
    lane = lax.broadcasted_iota(jnp.int32, (40, 256), 1)
    used = (lane < 144) | (lane >= 240)
    place = jnp.where(lane >= 192, lane - 256, lane) + gz * 128
    inside = used & (row >= 0) & (row < NY) & (place >= 0) & (place < NZ)
    b_full = jnp.where(inside, 2.0 / 7.0, 0.0).astype(f32)
    lane8 = lax.broadcasted_iota(jnp.int32, (8, 128), 1)
    tail_used = (lane8 < 16) | (lane8 >= 112)
    zero_plane = jnp.zeros((40, 256), f32)
    for ref in (even, odd):
        ref[0] = zero_plane
        ref[NX + 1] = zero_plane

    def fill(x, carry):
        chip, k = x // 4, x % 4
        amount = 112 - 32 * k
        for n, ref in enumerate((ym2_ref, ym1_ref, mid_ref, yp1_ref, yp2_ref)):
            rows = pl.ds(8 * n, 8)
            inner = b_full[8 * n:8 * n + 8]
            tail = pltpu.roll(ref[chip, 8], amount, 1)
            even[x + 1, rows, 0:128] = ref[chip, k]
            even[x + 1, rows, 128:256] = jnp.where(tail_used, tail, 0.0)
            tail = pltpu.roll(ref[chip, 9], amount, 1)
            coef[x, rows, 0:128] = (ref[chip, 4 + k] - 1.0) * inner[:, 0:128]
            coef[x, rows, 128:256] = (tail - 1.0) * inner[:, 128:256]
        return carry

    lax.fori_loop(0, NX, fill, 0)

    def put(pair, first, second):
        chip, k = pair // 2, 2 * (pair % 2)
        block = jnp.concatenate([first * mid_ref[chip, 10 + k], second * mid_ref[chip, 11 + k]], axis=0)
        high, middle, low = split_3(block)
        rows = pl.ds(pl.multiple_of(pair * 16, 16), 16)
        lhs[rows, 0:128] = middle
        lhs[rows, 128:256] = high
        lhs[rows, 256:384] = low

    def project(m):
        total = jnp.dot(lhs[:, 0:256], t1_ref[...], preferred_element_type=f32)
        total += jnp.dot(lhs[:, 0:256], t2_ref[...], preferred_element_type=f32)
        total += jnp.dot(lhs[:, 128:384], t3_ref[...], preferred_element_type=f32)
        part_ref[m:m + 1, :] = jnp.sum(total * w_ref[...], axis=0, keepdims=True)

    def keep(m, ref):
        def one(p, carry):
            plane = jnp.clip(4 * gx - 7 + p, 0, NX + 1)
            kept_ref[m, p] = ref[plane, 8:32, :]
            return carry
        lax.fori_loop(0, 20, one, 0)

    def keep_coef(p, carry):
        x = 4 * gx - 8 + p
        real = ((x >= 0) & (x < NX)).astype(f32)
        ka_ref[p] = coef[jnp.clip(x, 0, NX - 1), 8:32, :] * real
        kb_ref[p] = b_full[8:32] * real
        return carry

    lax.fori_loop(0, 20, keep_coef, 0)

    def first_put(pair, carry):
        put(pair, even[2 * pair + 1, 16:24, 0:128], even[2 * pair + 2, 16:24, 0:128])
        return carry

    lax.fori_loop(0, NX // 2, first_put, 0)
    project(0)
    keep(0, even)
    now, other = even, odd
    for m in range(1, DEGREE + 1):
        low, high = (0, 40) if m <= BASIS else (8, 32)
        own = slice(16 - low, 24 - low)
        b = b_full[low:high]

        def step(pair, carry, m=m, low=low, high=high, own=own, b=b, now=now, other=other):
            x = 2 * pair
            p0, p1, p2, p3 = [now[x + k, low:high, :] for k in range(4)]
            results = []
            for k, (before, here, after) in enumerate(((p0, p1, p2), (p1, p2, p3))):
                beside = around(before + after, here)
                value = coef[x + k, low:high, :] * here - b * beside
                value = 0.5 * value if m == 1 else value - other[x + k + 1, low:high, :]
                other[x + k + 1, low:high, :] = value
                results.append(value[own, 0:128])
            put(pair, *results)
            return carry

        lax.fori_loop(0, NX // 2, step, 0)
        project(m)
        if m <= BASIS:
            keep(m, other)
        now, other = other, now


def total_of(value):
    return jnp.sum(jnp.sum(value, axis=0, keepdims=True), axis=1, keepdims=True)


def dot_of(left, right):
    product = left * right
    half = product.shape[1] // 2
    return total_of(product[:, :half] + product[:, half:])


def images_of(vectors):
    out = [7.0 * (vectors[0] + vectors[1])]
    for k in range(1, BASIS):
        out.append(7.0 * vectors[k] + 3.5 * (vectors[k + 1] + vectors[k - 1]))
    return out


def solve(columns, target):
    columns = list(columns)
    basis, upper, overlap, inverse = [], {}, {}, []
    for j in range(BASIS):
        column = columns[j]
        if j:
            seen = [dot_of(basis[i], column) for i in range(j)]
            amounts = []
            for i in range(j):
                amount = seen[i]
                for k in range(i):
                    amount = amount - amounts[k] * overlap[i, k]
                amounts.append(amount)
            for i in range(j):
                column = column - amounts[i] * basis[i]
                upper[i, j] = upper[i, j] + amounts[i]
        length = jnp.sqrt(dot_of(column, column) + tiny_value)
        inverse.append(1.0 / length)
        basis.append(column * inverse[j])
        for later in range(j + 1, BASIS):
            amount = dot_of(basis[j], columns[later])
            columns[later] = columns[later] - amount * basis[j]
            upper[j, later] = amount
        for k in range(j):
            overlap[j, k] = dot_of(basis[j], basis[k])
    solved = [dot_of(vector, target) for vector in basis]
    for i in range(BASIS - 1, -1, -1):
        solved[i] = solved[i] * inverse[i]
        for k in range(i):
            solved[k] = solved[k] - upper[k, i] * solved[i]
    return solved


def remainder_of(solved):
    out = [-7.0 * c for c in solved] + [jnp.zeros_like(solved[0])]
    out[0] = out[0] + 1.0
    out[1] = out[1] - 7.0 * solved[0]
    for k in range(1, BASIS):
        out[k + 1] = out[k + 1] - 3.5 * solved[k]
        out[k - 1] = out[k - 1] - 3.5 * solved[k]
    return out


def finish_kernel(rows_ref, kept_ref, ka_ref, kb_ref, sol_ref, res_ref, even, odd):
    rows = [rows_ref[m] for m in range(DEGREE + 1)]
    first = solve(images_of(rows[:BASIS + 1]), rows[0])
    rest = remainder_of(first)
    turned = []
    for j in range(BASIS + 1):
        value = rest[0] * rows[j]
        for m in range(1, BASIS + 1):
            value = value + (0.5 * rest[m]) * (rows[m + j] + rows[abs(m - j)])
        turned.append(value)
    second = solve(images_of(turned), turned[0])
    last = remainder_of(second)

    zero_plane = jnp.zeros((24, 256), f32)
    for ref in (even, odd):
        ref[0] = zero_plane
        ref[21] = zero_plane

    def start(p, carry):
        value = rest[0] * kept_ref[0, p]
        for m in range(1, BASIS + 1):
            value = value + rest[m] * kept_ref[m, p]
        even[p + 1] = value
        return carry

    lax.fori_loop(0, 20, start, 0)
    for p in range(4):
        value = first[0] * kept_ref[0, 8 + p, 8:16, 0:128]
        for m in range(1, BASIS):
            value = value + first[m] * kept_ref[m, 8 + p, 8:16, 0:128]
        here = even[9 + p, 8:16, 0:128]
        sol_ref[p] = value + second[0] * here
        res_ref[p] = last[0] * here
    now, other = even, odd
    for m in range(1, BASIS + 1):
        def step(p, carry, m=m, now=now, other=other):
            here = now[p + 1]
            beside = around(now[p] + now[p + 2], here)
            value = ka_ref[p] * here - kb_ref[p] * beside
            other[p + 1] = 0.5 * value if m == 1 else value - other[p + 1]
            return carry

        lax.fori_loop(m, 20 - m, step, 0)
        for p in range(4):
            here = other[9 + p, 8:16, 0:128]
            if m < BASIS:
                sol_ref[p] += second[m] * here
            res_ref[p] += last[m] * here
        now, other = other, now


def run_basis(at, mid, sides, tables, weights, interpret=False):
    return pl.pallas_call(
        basis_kernel,
        out_shape=[
            jax.ShapeDtypeStruct((DEGREE + 1, SHARE), f32),
            jax.ShapeDtypeStruct((BASIS + 1, 20, 24, 256), f32),
            jax.ShapeDtypeStruct((20, 24, 256), f32),
            jax.ShapeDtypeStruct((20, 24, 256), f32),
        ],
        in_specs=[pl.BlockSpec(memory_space=pltpu.SMEM)] + [pl.BlockSpec(memory_space=VMEM)] * 9,
        out_specs=[pl.BlockSpec(memory_space=VMEM)] * 4,
        scratch_shapes=[
            VMEM((NX + 2, 40, 256), f32),
            VMEM((NX + 2, 40, 256), f32),
            VMEM((NX, 40, 256), f32),
            VMEM((256, 384), bf16),
        ],
        name="basis",
        interpret=interpret,
    )(at, mid, *sides, *tables, weights)


def run_finish(rows, kept, ka, kb, interpret=False):
    return pl.pallas_call(
        finish_kernel,
        out_shape=[jax.ShapeDtypeStruct((4, 8, 128), f32)] * 2,
        in_specs=[pl.BlockSpec(memory_space=VMEM)] * 4,
        out_specs=[pl.BlockSpec(memory_space=VMEM)] * 2,
        scratch_shapes=[VMEM((22, 24, 256), f32), VMEM((22, 24, 256), f32)],
        name="finish",
        interpret=interpret,
    )(rows, kept, ka, kb)


def prepared_tables(freq_x, freq_y, freq_z, gx, gy, gz):
    mine = [lax.dynamic_slice_in_dim(f, gx * SHARE, SHARE) for f in (freq_x, freq_y, freq_z)]
    table_x = cosine_table(mine[0], 0, NX, NX)
    table_y = cosine_table(mine[1], gy * 8, 8, NY)
    table_z = cosine_table(mine[2], gz * 128, 128, NZ)
    high, middle, low = split_3(table_z)
    tables = [jnp.concatenate(pair, axis=0) for pair in ((high, high), (middle, middle), (low, high))]
    weights = (table_x[:, None, :] * table_y[None, :, :]).reshape(NX * 8, SHARE)
    return tables, weights


def to_all(value, axis, size):
    return lax.all_to_all(
        jnp.broadcast_to(value[None], (size, *value.shape)), axis, 0, 0, tiled=True
    )


def tail_of(before, after):
    pieces = []
    for k in range(4):
        pieces += [before[:, k], after[:, k]]
    return jnp.concatenate(pieces, axis=-1)


def shards(right_side, diagonal, sign_bits, freq_x, freq_y, freq_z):
    gx, gy, gz = lax.axis_index("gx"), lax.axis_index(GY), lax.axis_index("gz")
    both = jnp.stack([right_side, diagonal])
    before = shifted(both[..., -16:], "gz", GZ, 1)
    after = shifted(both[..., :16], "gz", GZ, -1)
    signs = 1.0 - 2.0 * sign_bits.astype(f32)
    sent = jnp.concatenate([both.reshape(8, 8, 128), tail_of(before, after), signs], axis=0)
    mid = to_all(sent, "gx", GX)
    shared = mid[:, :10]
    sides = [shifted(shared, GY, 16, by) for by in (2, 1, -1, -2)]
    tables, weights = prepared_tables(freq_x, freq_y, freq_z, gx, gy, gz)
    at = jnp.stack([gx, gy, gz]).astype(jnp.int32)
    part, kept, ka, kb = run_basis(at, mid, sides, tables, weights)
    rows = reduced(part)
    return tuple(run_finish(rows, kept, ka, kb))


def reduced(part):
    pieces = part.reshape(17, GZ, 32).transpose(1, 0, 2).reshape(GZ, 544)
    pieces = lax.all_to_all(pieces, "gz", 0, 0, tiled=True).sum(axis=0)
    pieces = to_all(pieces, GY, 16).sum(axis=0)
    pieces = to_all(pieces, ("gx", "gz"), GX * GZ)
    return pieces.reshape(8, 8, 17, 32).transpose(2, 0, 1, 3).reshape(17, 8, 256)


def solution(mesh):
    split = Mesh(
        mesh.devices.reshape(mesh.shape["gx"], 8, 2, mesh.shape["gz"]), ("gx", "gy_0", "gy_1", "gz")
    )
    return jax.shard_map(
        shards,
        mesh=split,
        in_specs=(P("gx", GY, "gz"), P("gx", GY, "gz"), P("gx", GY, "gz"), P(), P(), P()),
        out_specs=(P("gx", GY, "gz"), P("gx", GY, "gz")),
        check_vma=False,
    )
```

time: 771 us -> 171 us (0.22); the launches traced: 758 us -> 171 us
  starting transfers between devices: 267 us -> 35.9 us
  blocking collectives: 194 us -> 47.1 us
  other arithmetic: 140 us -> 5.86 us
  between operations: 96.9 us -> 0.84 us
  Pallas kernels: 0 us -> 56.9 us
  waiting for transfers between devices: 44.6 us -> 17.8 us
  matrix products: 8 us -> 0 us
    ppermute x90 -> x6, starting transfers between devices: 267 us -> 19.5 us  [shifted(): return lax.ppermute(value, axis_name, pairs)]
    psum x6 -> x0, blocking collectives: 130 us -> none  [one_axis_at_a_time(): shard = lax.psum(shard, axis)]
    sub x77 -> x1, other arithmetic: 73 us -> 0.72 us  [shards(): signs = 1.0 - 2.0 * sign_bits.astype(f32)]
    pallas_call x0 -> x2, Pallas kernels: none -> 56.9 us  [the longest x1 41.3 us: run_basis(): pl.pallas_call(basis_kernel, out_shape=[jax.ShapeDtypeStruct((DEGREE + 1,...]
    dot_general x88 -> x0, other arithmetic: 56.4 us -> none  [the longest x68 44.1 us: least_squares(): amount = jnp.dot(orthonormal[earlier], column, precision=highest)]
    ppermute x90 -> x6, waiting for transfers between devices: 44.6 us -> 8.32 us  [shifted(): return lax.ppermute(value, axis_name, pairs)]
    all_to_all x4 -> x3, blocking collectives: 64.1 us -> 47.1 us  [the longest x2 33.3 us: to_all(): lax.all_to_all(jnp.broadcast_to(value[None], (size, *value.shape)), axis,...]
    all_to_all x0 -> x1, starting transfers between devices: none -> 16.4 us  [to_all(): lax.all_to_all(jnp.broadcast_to(value[None], (size, *value.shape)), axis,...]
  transfers between devices with their start and end apart: 90 -> 7, of which waited for: 12 -> 3; matrix products, arithmetic and copies ran while one was open for 1% -> 4% of each run, Pallas kernels for 0% -> 0%
where the time goes in v1:
time: 171 us
  Pallas kernels  56.9 us (33%)
  blocking collectives  47.1 us (28%)
  starting transfers between devices  35.9 us (21%)
  waiting for transfers between devices  17.8 us (10%)
  local copies, waits for them, and re-layouts  6.11 us (4%)
  other arithmetic  5.86 us (3%)
    pallas_call x1, Pallas kernels, run_basis(): pl.pallas_call(basis_kernel, out_shape=[jax.ShapeDtypeStruct((DEGREE + 1,...  41.3 us
    all_to_all x2, blocking collectives, to_all(): lax.all_to_all(jnp.broadcast_to(value[None], (size, *value.shape)), axis,...  33.3 us
    ppermute x6, starting transfers between devices, shifted(): return lax.ppermute(value, axis_name, pairs)  19.5 us
    all_to_all x1, starting transfers between devices, to_all(): lax.all_to_all(jnp.broadcast_to(value[None], (size, *value.shape)), axis,...  16.4 us
    pallas_call x1, Pallas kernels, run_finish(): pl.pallas_call(finish_kernel, out_shape=[jax.ShapeDtypeStruct((4, 8, 128)...  15.6 us
    all_to_all x1, blocking collectives, reduced(): pieces = lax.all_to_all(pieces, 'gz', 0, 0, tiled=True).sum(axis=0)  13.8 us
    all_to_all x1, waiting for transfers between devices, to_all(): lax.all_to_all(jnp.broadcast_to(value[None], (size, *value.shape)), axis,...  9.53 us
    ppermute x6, waiting for transfers between devices, shifted(): return lax.ppermute(value, axis_name, pairs)  8.32 us
  transfers between devices with their start and end apart: 7, of which 3 were waited for; matrix products, arithmetic and copies ran while one was open for 4% of the time, Pallas kernels for 0%

profile of v1, /device:TPU:1, one launch (start us, length us, event | category | flops | bytes accessed | tf_op | source)
XLA Modules:
  0.0 170.6 jit_solution(11980926966628264541)
XLA Ops:
  0.6 0.9 fusion.8
  1.5 4.1 %collective-permute-start = (f32[2,4,8,16]{3,2,0,1:T(8,128)S(1)}, f32[2,4,8,16]{3,2,0,1:T(8,128)S(1)}, u32[]{:S(2)}, u32[]{:S(2)}) collective-permute-start(f32[2,4,8,16]{3,2,0,1:T(8,128)S(1)} %copy.41), channel_id=1, source_target_pairs={{0,1},{1,2},{2,3},{3,4},{4,5},{5,6},{6,7},{8,9},{9,10},{10,11},{11... | collective-permute-start | bytes 12296 | tf_op jit(solution)/shard_map/ppermute | solution.py:22
  5.6 1.3 collective-permute-start.1
  7.0 0.7 pad_maximum_fusion.4
  7.7 0.7 multiply_subtract_fusion
  8.5 1.8 %collective-permute-done.1 = f32[2,4,8,16]{3,2,1,0:T(8,128)S(1)} collective-permute-done((f32[2,4,8,16]{3,2,1,0:T(8,128)S(1)}, f32[2,4,8,16]{3,2,1,0:T(8,128)S(1)}, u32[]{:S(2)}, u32[]{:S(2)}) %collective-permute-start.1) | collective-permute-done | bytes 4128 | tf_op jit(solution)/shard_map/ppermute | solution.py:22
  10.4 0.8 broadcast_in_dim.6
  11.2 16.4 %all-to-all-start = ((f32[8,14,8,128]{3,2,1,0:T(8,128)}), f32[8,14,8,128]{3,2,1,0:T(8,128)S(1)}, u32[]{:S(2)}, u32[]{:S(2)}) async-start(f32[8,14,8,128]{3,2,1,0:T(8,128)} %broadcast_in_dim.6), calls=%async_computation | async-start | bytes 917504 | tf_op jit(solution)/shard_map/all_to_all | solution.py:298
  27.6 0.8 dynamic_slice.10
  28.4 0.8 dynamic_slice.11
  29.1 0.8 dynamic_slice.9
  29.9 0.6 subtract_convert_fusion
  30.5 0.8 pad_maximum_fusion
  31.4 0.2 fusion.12
  31.6 9.5 %all-to-all-done.mid_ref = f32[8,14,8,128]{3,2,1,0:T(8,128)S(1)} async-done(((f32[8,14,8,128]{3,2,1,0:T(8,128)}), f32[8,14,8,128]{3,2,1,0:T(8,128)S(1)}, u32[]{:S(2)}, u32[]{:S(2)}) %all-to-all-start) | async-done | bytes 458784 | tf_op jit(solution)/shard_map/all_to_all | solution.py:298
  41.2 1.3 collective-permute-start.5
  42.5 5.4 %collective-permute-start.4 = (f32[8,10,8,128]{3,2,1,0:T(8,128)S(1)}, f32[8,10,8,128]{3,2,1,0:T(8,128)S(1)}, u32[]{:S(2)}, u32[]{:S(2)}) collective-permute-start(f32[8,10,8,128]{3,2,1,0:T(8,128)S(1)} %slice.56), channel_id=1, source_target_pairs={{8,0},{16,8},{24,16},{32,24},{40,32},{48,40},{56,48},{64,56},{72,6... | collective-permute-start | bytes 983048 | tf_op jit(solution)/shard_map/ppermute | solution.py:22
  47.9 4.2 %collective-permute-start.3 = (f32[8,10,8,128]{3,2,1,0:T(8,128)S(1)}, f32[8,10,8,128]{3,2,1,0:T(8,128)S(1)}, u32[]{:S(2)}, u32[]{:S(2)}) collective-permute-start(f32[8,10,8,128]{3,2,1,0:T(8,128)S(1)} %slice.56), channel_id=1, source_target_pairs={{0,8},{8,16},{16,24},{24,32},{32,40},{40,48},{48,56},{56,64},{64,7... | collective-permute-start | bytes 983048 | tf_op jit(solution)/shard_map/ppermute | solution.py:22
  52.1 3.1 %collective-permute-start.2 = (f32[8,10,8,128]{3,2,1,0:T(8,128)S(1)}, f32[8,10,8,128]{3,2,1,0:T(8,128)S(1)}, u32[]{:S(2)}, u32[]{:S(2)}) collective-permute-start(f32[8,10,8,128]{3,2,1,0:T(8,128)S(1)} %slice.56), channel_id=1, source_target_pairs={{0,16},{8,24},{16,32},{24,40},{32,48},{40,56},{48,64},{56,72},{64,... | collective-permute-start | bytes 983048 | tf_op jit(solution)/shard_map/ppermute | solution.py:22
  55.2 0.7 pad_add_fusion.at_ref
  55.9 0.7 multiply_bitcast_fusion.w_ref
  56.6 6.5 %collective-permute-done.2.ym2_ref = f32[8,10,8,128]{3,2,1,0:T(8,128)S(1)} collective-permute-done((f32[8,10,8,128]{3,2,1,0:T(8,128)S(1)}, f32[8,10,8,128]{3,2,1,0:T(8,128)S(1)}, u32[]{:S(2)}, u32[]{:S(2)}) %collective-permute-start.2) | collective-permute-done | bytes 327712 | tf_op jit(solution)/shard_map/ppermute | solution.py:22
  63.1 0.7 copy-done.4
  63.8 41.3 %basis.1 = (f32[17,256]{1,0:T(8,128)}, f32[9,20,24,256]{3,2,1,0:T(8,128)}, f32[20,24,256]{2,1,0:T(8,128)}, f32[20,24,256]{2,1,0:T(8,128)}) custom-call(s32[3]{0:T(128)} %pad_add_fusion.at_ref, f32[8,14,8,128]{3,2,1,0:T(8,128)} %copy-done, f32[8,10,8,128]{3,2,1,0:T(8,128)} %copy-done.4, f32[8,10,8,128]{3,2,1,0:T(8,128)} %copy-done.3, ...), custom_call_target="tpu_custom_call" | custom-call | tf_op jit(solution)/shard_map/basis/pallas_call | solution.py:253
  105.1 0.8 reshape.144
  106.1 13.8 %all_to_all.27 = f32[8,1,544]{2,1,0:T(1,128)S(1)} all-to-all(f32[8,1,544]{2,1,0:T(1,128)S(1)} %all_to_all.22), channel_id=1, replica_groups=mesh['gx'=8,'gy_0'=8,'gy_1'=2,'gz'=8] {'gz'}, dimensions={0} | all-to-all | bytes 34816 | tf_op jit(solution)/shard_map/all_to_all | solution.py:329
  119.9 17.5 %all_to_all.28 = f32[16,1,544]{2,1,0:T(1,128)S(1)} all-to-all(f32[16,1,544]{2,1,0:T(1,128)S(1)} %broadcast_in_dim.7), channel_id=1, replica_groups=mesh['gx'=8,'gy_0'=8,'gy_1'=2,'gz'=8] {'gy_0','gy_1'}, dimensions={0} | all-to-all | bytes 69632 | tf_op jit(solution)/shard_map/all_to_all | solution.py:298
  137.6 15.8 %all_to_all.29 = f32[64,1,544]{2,1,0:T(1,128)S(1)} all-to-all(f32[64,1,544]{2,1,0:T(1,128)S(1)} %broadcast_in_dim.8), channel_id=1, replica_groups=mesh['gx'=8,'gy_0'=8,'gy_1'=2,'gz'=8] {'gx','gz'}, dimensions={0} | all-to-all | bytes 278528 | tf_op jit(solution)/shard_map/all_to_all | solution.py:298
  153.4 0.4 reduce.2
  153.8 0.2 reshape.145
  154.1 0.9 reshape.146.rows_ref
  154.9 15.6 %finish.1 = (f32[4,8,128]{2,1,0:T(8,128)}, f32[4,8,128]{2,1,0:T(8,128)}) custom-call(f32[17,8,256]{2,1,0:T(8,128)} %reshape.146.rows_ref, f32[9,20,24,256]{3,2,1,0:T(8,128)} %get-tuple-element.7.kept_ref, f32[20,24,256]{2,1,0:T(8,128)} %get-tuple-element.8.ka_ref, f32[20,24,256]{2,1,0:T(8,128)} %get-tuple-element.9.kb_ref), custom_call_target="tpu_custom_call" | custom-call | tf_op jit(solution)/shard_map/finish/pallas_call | solution.py:275
  (30 shorter events, 0.7 us)
Async XLA Ops:
  1.5 6.9 %collective-permute-start = (f32[2,4,8,16]{3,2,0,1:T(8,128)S(1)}, f32[2,4,8,16]{3,2,0,1:T(8,128)S(1)}, u32[]{:S(2)}, u32[]{:S(2)}) collective-permute-start(f32[2,4,8,16]{3,2,0,1:T(8,128)S(1)} %copy.41), channel_id=1, source_target_pairs={{0,1},{1,2},{2,3},{3,4},{4,5},{5,6},{6,7},{8,9},{9,10},{10,11},{11... | collective-permute-start | bytes 12296 | tf_op jit(solution)/shard_map/ppermute | solution.py:22
  5.6 4.7 %collective-permute-start.1 = (f32[2,4,8,16]{3,2,1,0:T(8,128)S(1)}, f32[2,4,8,16]{3,2,1,0:T(8,128)S(1)}, u32[]{:S(2)}, u32[]{:S(2)}) collective-permute-start(f32[2,4,8,16]{3,2,1,0:T(8,128)S(1)} %get-tuple-element.20), channel_id=1, source_target_pairs={{1,0},{2,1},{3,2},{4,3},{5,4},{6,5},{7,6},{9,8},{10,9},{11,10},{12... | collective-permute-start | bytes 12296 | tf_op jit(solution)/shard_map/ppermute | solution.py:22
  11.2 29.9 %all-to-all-start = ((f32[8,14,8,128]{3,2,1,0:T(8,128)}), f32[8,14,8,128]{3,2,1,0:T(8,128)S(1)}, u32[]{:S(2)}, u32[]{:S(2)}) async-start(f32[8,14,8,128]{3,2,1,0:T(8,128)} %broadcast_in_dim.6), calls=%async_computation | async-start | bytes 917504 | tf_op jit(solution)/shard_map/all_to_all | solution.py:298
  41.1 22.0 %copy-start = (f32[8,14,8,128]{3,2,1,0:T(8,128)}, f32[8,14,8,128]{3,2,1,0:T(8,128)S(1)}, u32[]{:S(2)}) copy-start(f32[8,14,8,128]{3,2,1,0:T(8,128)S(1)} %all-to-all-done.mid_ref) | copy-start | bytes 1376260
  41.2 15.4 %collective-permute-start.5 = (f32[8,10,8,128]{3,2,1,0:T(8,128)S(1)}, f32[8,10,8,128]{3,2,1,0:T(8,128)S(1)}, u32[]{:S(2)}, u32[]{:S(2)}) collective-permute-start(f32[8,10,8,128]{3,2,1,0:T(8,128)S(1)} %slice.56), channel_id=1, source_target_pairs={{16,0},{24,8},{32,16},{40,24},{48,32},{56,40},{64,48},{72,56},{80,... | collective-permute-start | bytes 983048 | tf_op jit(solution)/shard_map/ppermute | solution.py:22
  42.5 14.1 %collective-permute-start.4 = (f32[8,10,8,128]{3,2,1,0:T(8,128)S(1)}, f32[8,10,8,128]{3,2,1,0:T(8,128)S(1)}, u32[]{:S(2)}, u32[]{:S(2)}) collective-permute-start(f32[8,10,8,128]{3,2,1,0:T(8,128)S(1)} %slice.56), channel_id=1, source_target_pairs={{8,0},{16,8},{24,16},{32,24},{40,32},{48,40},{56,48},{64,56},{72,6... | collective-permute-start | bytes 983048 | tf_op jit(solution)/shard_map/ppermute | solution.py:22
  47.9 8.7 %collective-permute-start.3 = (f32[8,10,8,128]{3,2,1,0:T(8,128)S(1)}, f32[8,10,8,128]{3,2,1,0:T(8,128)S(1)}, u32[]{:S(2)}, u32[]{:S(2)}) collective-permute-start(f32[8,10,8,128]{3,2,1,0:T(8,128)S(1)} %slice.56), channel_id=1, source_target_pairs={{0,8},{8,16},{16,24},{24,32},{32,40},{40,48},{48,56},{56,64},{64,7... | collective-permute-start | bytes 983048 | tf_op jit(solution)/shard_map/ppermute | solution.py:22
  52.1 11.0 %collective-permute-start.2 = (f32[8,10,8,128]{3,2,1,0:T(8,128)S(1)}, f32[8,10,8,128]{3,2,1,0:T(8,128)S(1)}, u32[]{:S(2)}, u32[]{:S(2)}) collective-permute-start(f32[8,10,8,128]{3,2,1,0:T(8,128)S(1)} %slice.56), channel_id=1, source_target_pairs={{0,16},{8,24},{16,32},{24,40},{32,48},{40,56},{48,64},{56,72},{64,... | collective-permute-start | bytes 983048 | tf_op jit(solution)/shard_map/ppermute | solution.py:22
  56.6 6.5 %copy-start.1 = (f32[8,10,8,128]{3,2,1,0:T(8,128)}, f32[8,10,8,128]{3,2,1,0:T(8,128)S(1)}, u32[]{:S(2)}) copy-start(f32[8,10,8,128]{3,2,1,0:T(8,128)S(1)} %collective-permute-done.5.yp2_ref) | copy-start | bytes 983044
  56.6 6.5 %copy-start.2 = (f32[8,10,8,128]{3,2,1,0:T(8,128)}, f32[8,10,8,128]{3,2,1,0:T(8,128)S(1)}, u32[]{:S(2)}) copy-start(f32[8,10,8,128]{3,2,1,0:T(8,128)S(1)} %collective-permute-done.4.yp1_ref) | copy-start | bytes 983044
  56.6 6.5 %copy-start.3 = (f32[8,10,8,128]{3,2,1,0:T(8,128)}, f32[8,10,8,128]{3,2,1,0:T(8,128)S(1)}, u32[]{:S(2)}) copy-start(f32[8,10,8,128]{3,2,1,0:T(8,128)S(1)} %collective-permute-done.3.ym1_ref) | copy-start | bytes 983044
  63.1 0.7 copy-start.4

commit v2 on v1

v2 whole, which is shorter than its diff:
```python
import jax
import jax.numpy as jnp
from jax import lax
from jax.experimental import pallas as pl
from jax.experimental.pallas import tpu as pltpu
from jax.sharding import Mesh
from jax.sharding import PartitionSpec as P

BASIS = 8
DEGREE = 2 * BASIS
NX, NY, NZ, SKETCH = 32, 128, 1024, 2048
GX, GZ = 8, 8
SHARE = SKETCH // GX
GY = ("gy_0", "gy_1")
tiny_value = 1e-06
VMEM = pltpu.VMEM
f32, bf16 = jnp.float32, jnp.bfloat16


def shifted(value, axis_name, size, by):
    pairs = [(i, i + by) for i in range(size) if 0 <= i + by < size]
    return lax.ppermute(value, axis_name, pairs)


def cosine_table(freqs, offset, count, length):
    indices = offset + jnp.arange(count, dtype=jnp.int32)
    phases = (2 * indices[:, None] + 1) * freqs[None, :] % (4 * length)
    return (jnp.sqrt(2.0 / length) * jnp.cos(jnp.pi * phases / (2.0 * length))).astype(f32)


def split_3(value):
    high = value.astype(bf16)
    rest = value - high.astype(f32)
    middle = rest.astype(bf16)
    low = (rest - middle.astype(f32)).astype(bf16)
    return high, middle, low


def beside_z(halves):
    lane = lax.broadcasted_iota(jnp.int32, halves[0].shape, 1)
    low = [pltpu.roll(half, 1, 1) for half in halves]
    high = [pltpu.roll(half, 127, 1) for half in halves]
    return [
        jnp.where(lane == 0, low[1 - h], low[h]) + jnp.where(lane == 127, high[1 - h], high[h])
        for h in range(2)
    ]


def next_plane(now, other, coef, scale, x, rows, first, at=None):
    low, high = rows
    at = x if at is None else at
    here = [now[x + 1, h, low:high, :] for h in range(2)]
    sides = beside_z(here)
    out = []
    for h in range(2):
        total = now[x, h, low:high, :] + now[x + 2, h, low:high, :]
        total = total + (now[x + 1, h, low - 1:high - 1, :] + now[x + 1, h, low + 1:high + 1, :])
        total = total + sides[h]
        value = coef[at, h, low - 8:high - 8, :] * here[h] - scale(h) * total
        value = 0.5 * value if first else value - other[x + 1, h, low:high, :]
        other[x + 1, h, low:high, :] = value
        out.append(value)
    return out


def basis_kernel(at_ref, mid_ref, ym2_ref, ym1_ref, yp1_ref, yp2_ref, table_ref, w_ref,
                 part_ref, kept_ref, ka_ref, kb_ref, even, odd, coef, mask, lhs):
    gx, gy, gz = at_ref[0], at_ref[1], at_ref[2]
    row = lax.broadcasted_iota(jnp.int32, (40, 128), 0) - 16 + gy * 8
    lane = lax.broadcasted_iota(jnp.int32, (40, 128), 1)
    rows_in = (row >= 0) & (row < NY)
    mask[0] = jnp.where(rows_in, 2.0 / 7.0, 0.0).astype(f32)
    place = jnp.where(lane >= 64, lane - 128, lane + 128) + gz * 128
    tail_in = rows_in & ((lane < 16) | (lane >= 112)) & (place >= 0) & (place < NZ)
    mask[1] = jnp.where(tail_in, 2.0 / 7.0, 0.0).astype(f32)
    lane8 = lax.broadcasted_iota(jnp.int32, (8, 128), 1)
    tail_used = (lane8 < 16) | (lane8 >= 112)
    empty = jnp.zeros((8, 128), f32)
    for ref in (even, odd):
        for plane in (0, NX + 1):
            for h in range(2):
                ref[plane, h] = jnp.zeros((56, 128), f32)

    def fill(chip, carry):
        for k in range(4):
            x = 4 * chip + k
            for h in range(2):
                for ref in (even, odd):
                    ref[x + 1, h, 0:8, :] = empty
                    ref[x + 1, h, 48:56, :] = empty
            for n, ref in enumerate((ym2_ref, ym1_ref, mid_ref, yp1_ref, yp2_ref)):
                rows = slice(8 * n, 8 * n + 8)
                padded = slice(8 * n + 8, 8 * n + 16)
                even[x + 1, 0, padded, :] = ref[chip, k]
                tail = pltpu.roll(ref[chip, 8], 112 - 32 * k, 1)
                even[x + 1, 1, padded, :] = jnp.where(tail_used, tail, 0.0)
                coef[x, 0, rows, :] = (ref[chip, 4 + k] - 1.0) * mask[0, rows, :]
                tail = pltpu.roll(ref[chip, 9], 112 - 32 * k, 1)
                coef[x, 1, rows, :] = (tail - 1.0) * mask[1, rows, :]
        return carry

    lax.fori_loop(0, GX, fill, 0)

    def put(m, chip, k, first, second):
        block = jnp.concatenate([first * mid_ref[chip, 10 + k], second * mid_ref[chip, 11 + k]], axis=0)
        high, middle, low = split_3(block)
        rows = pl.ds(pl.multiple_of(256 * (m % 2) + 32 * chip + 8 * k, 16), 16)
        lhs[rows, 0:128] = middle
        lhs[rows, 128:256] = high
        lhs[rows, 256:384] = low

    def project(begin, end):
        size = 256 * (end - begin)
        rows = lhs[0:size, :]
        stacked = jnp.concatenate([rows[:, 0:256], rows[:, 0:256], rows[:, 128:384]], axis=1)
        total = jnp.dot(stacked, table_ref[...], preferred_element_type=f32)
        for m in range(begin, end):
            own = total[256 * (m - begin):256 * (m - begin + 1)]
            part_ref[m:m + 1, :] = jnp.sum(own * w_ref[...], axis=0, keepdims=True)

    def keep(m, ref):
        def one(p, carry):
            plane = jnp.clip(4 * gx - 7 + p, 0, NX + 1)
            kept_ref[m, p] = ref[plane, :, 16:40, :]
            return carry
        lax.fori_loop(0, 20, one, 0, unroll=4)

    def keep_coef(p, carry):
        x = 4 * gx - 8 + p
        real = ((x >= 0) & (x < NX)).astype(f32)
        ka_ref[p] = coef[jnp.clip(x, 0, NX - 1), :, 8:32, :] * real
        kb_ref[p] = mask[:, 8:32, :] * real
        return carry

    lax.fori_loop(0, 20, keep_coef, 0)

    def first_put(chip, carry):
        for k in (0, 2):
            put(0, chip, k, *[even[4 * chip + k + d + 1, 0, 24:32, :] for d in range(2)])
        return carry

    lax.fori_loop(0, GX, first_put, 0)
    keep(0, even)
    now, other = even, odd
    for m in range(1, DEGREE + 1):
        rows = (8, 48) if m <= BASIS else (16, 40)

        def step(chip, carry, m=m, rows=rows, now=now, other=other):
            own = slice(24 - rows[0], 32 - rows[0])
            for k in (0, 2):
                pair = []
                for d in range(2):
                    x = 4 * chip + k + d
                    scale = lambda h: mask[h, rows[0] - 8:rows[1] - 8, :]
                    pair.append(next_plane(now, other, coef, scale, x, rows, m == 1)[0][own])
                put(m, chip, k, *pair)
            return carry

        lax.fori_loop(0, GX, step, 0)
        if m % 2:
            project(m - 1, m + 1)
        if m <= BASIS:
            keep(m, other)
        now, other = other, now
    project(DEGREE, DEGREE + 1)


def total_of(value):
    return jnp.sum(jnp.sum(value, axis=0, keepdims=True), axis=1, keepdims=True)


def dot_of(left, right):
    product = left * right
    half = product.shape[1] // 2
    return total_of(product[:, :half] + product[:, half:])


def images_of(vectors):
    out = [7.0 * (vectors[0] + vectors[1])]
    for k in range(1, BASIS):
        out.append(7.0 * vectors[k] + 3.5 * (vectors[k + 1] + vectors[k - 1]))
    return out


def solve(columns, target):
    columns = list(columns)
    basis, upper, overlap, inverse = [], {}, {}, []
    for j in range(BASIS):
        column = columns[j]
        if j:
            seen = [dot_of(basis[i], column) for i in range(j)]
            amounts = []
            for i in range(j):
                amount = seen[i]
                for k in range(i):
                    amount = amount - amounts[k] * overlap[i, k]
                amounts.append(amount)
            for i in range(j):
                column = column - amounts[i] * basis[i]
                upper[i, j] = upper[i, j] + amounts[i]
        length = jnp.sqrt(dot_of(column, column) + tiny_value)
        inverse.append(1.0 / length)
        basis.append(column * inverse[j])
        for later in range(j + 1, BASIS):
            amount = dot_of(basis[j], columns[later])
            columns[later] = columns[later] - amount * basis[j]
            upper[j, later] = amount
        for k in range(j):
            overlap[j, k] = dot_of(basis[j], basis[k])
    solved = [dot_of(vector, target) for vector in basis]
    for i in range(BASIS - 1, -1, -1):
        solved[i] = solved[i] * inverse[i]
        for k in range(i):
            solved[k] = solved[k] - upper[k, i] * solved[i]
    return solved


def remainder_of(solved):
    out = [-7.0 * c for c in solved] + [jnp.zeros_like(solved[0])]
    out[0] = out[0] + 1.0
    out[1] = out[1] - 7.0 * solved[0]
    for k in range(1, BASIS):
        out[k + 1] = out[k + 1] - 3.5 * solved[k]
        out[k - 1] = out[k - 1] - 3.5 * solved[k]
    return out


def finish_kernel(rows_ref, kept_ref, ka_ref, kb_ref, sol_ref, res_ref, even, odd):
    rows = [rows_ref[m] for m in range(DEGREE + 1)]
    first = solve(images_of(rows[:BASIS + 1]), rows[0])
    rest = remainder_of(first)
    turned = []
    for j in range(BASIS + 1):
        value = rest[0] * rows[j]
        for m in range(1, BASIS + 1):
            value = value + (0.5 * rest[m]) * (rows[m + j] + rows[abs(m - j)])
        turned.append(value)
    second = solve(images_of(turned), turned[0])
    last = remainder_of(second)

    for ref in (even, odd):
        for h in range(2):
            ref[0, h] = jnp.zeros((40, 128), f32)
            ref[21, h] = jnp.zeros((40, 128), f32)

    def start(p, carry):
        for h in range(2):
            value = rest[0] * kept_ref[0, p, h]
            for m in range(1, BASIS + 1):
                value = value + rest[m] * kept_ref[m, p, h]
            even[p + 1, h, 8:32, :] = value
            for ref in (even, odd):
                ref[p + 1, h, 0:8, :] = jnp.zeros((8, 128), f32)
                ref[p + 1, h, 32:40, :] = jnp.zeros((8, 128), f32)
        return carry

    lax.fori_loop(0, 20, start, 0)
    for p in range(4):
        value = first[0] * kept_ref[0, 8 + p, 0, 8:16, :]
        for m in range(1, BASIS):
            value = value + first[m] * kept_ref[m, 8 + p, 0, 8:16, :]
        here = even[9 + p, 0, 16:24, :]
        sol_ref[p] = value + second[0] * here
        res_ref[p] = last[0] * here
    now, other = even, odd
    for m in range(1, BASIS + 1):
        def step(q, carry, m=m, now=now, other=other):
            for d in range(2):
                p = m + 2 * q + d
                scale = lambda h: kb_ref[p, h]
                next_plane(now, other, ka_ref, scale, p, (8, 32), m == 1)
            return carry

        lax.fori_loop(0, 10 - m, step, 0)
        for p in range(4):
            here = other[9 + p, 0, 16:24, :]
            if m < BASIS:
                sol_ref[p] += second[m] * here
            res_ref[p] += last[m] * here
        now, other = other, now


def run_basis(at, mid, sides, table, weights, interpret=False):
    return pl.pallas_call(
        basis_kernel,
        out_shape=[
            jax.ShapeDtypeStruct((DEGREE + 1, SHARE), f32),
            jax.ShapeDtypeStruct((BASIS + 1, 20, 2, 24, 128), f32),
            jax.ShapeDtypeStruct((20, 2, 24, 128), f32),
            jax.ShapeDtypeStruct((20, 2, 24, 128), f32),
        ],
        in_specs=[pl.BlockSpec(memory_space=pltpu.SMEM)] + [pl.BlockSpec(memory_space=VMEM)] * 7,
        out_specs=[pl.BlockSpec(memory_space=VMEM)] * 4,
        scratch_shapes=[
            VMEM((NX + 2, 2, 56, 128), f32),
            VMEM((NX + 2, 2, 56, 128), f32),
            VMEM((NX, 2, 40, 128), f32),
            VMEM((2, 40, 128), f32),
            VMEM((512, 384), bf16),
        ],
        compiler_params=pltpu.CompilerParams(vmem_limit_bytes=28 << 20),
        name="basis",
        interpret=interpret,
    )(at, mid, *sides, table, weights)


def run_finish(rows, kept, ka, kb, interpret=False):
    return pl.pallas_call(
        finish_kernel,
        out_shape=[jax.ShapeDtypeStruct((4, 8, 128), f32)] * 2,
        in_specs=[pl.BlockSpec(memory_space=VMEM)] * 4,
        out_specs=[pl.BlockSpec(memory_space=VMEM)] * 2,
        scratch_shapes=[VMEM((22, 2, 40, 128), f32), VMEM((22, 2, 40, 128), f32)],
        compiler_params=pltpu.CompilerParams(vmem_limit_bytes=28 << 20),
        name="finish",
        interpret=interpret,
    )(rows, kept, ka, kb)


def prepared_tables(freq_x, freq_y, freq_z, gx, gy, gz):
    mine = [lax.dynamic_slice_in_dim(f, gx * SHARE, SHARE) for f in (freq_x, freq_y, freq_z)]
    table_x = cosine_table(mine[0], 0, NX, NX)
    table_y = cosine_table(mine[1], gy * 8, 8, NY)
    table_z = cosine_table(mine[2], gz * 128, 128, NZ)
    high, middle, low = split_3(table_z)
    table = jnp.concatenate([high, high, middle, middle, low, high], axis=0)
    weights = (table_x[:, None, :] * table_y[None, :, :]).reshape(NX * 8, SHARE)
    return table, weights


def to_all(value, axis, size):
    return lax.all_to_all(
        jnp.broadcast_to(value[None], (size, *value.shape)), axis, 0, 0, tiled=True
    )


def tail_of(before, after):
    pieces = []
    for k in range(4):
        pieces += [before[:, k], after[:, k]]
    return jnp.concatenate(pieces, axis=-1)


def shards(right_side, diagonal, sign_bits, freq_x, freq_y, freq_z):
    gx, gy, gz = lax.axis_index("gx"), lax.axis_index(GY), lax.axis_index("gz")
    both = jnp.stack([right_side, diagonal])
    before = shifted(both[..., -16:], "gz", GZ, 1)
    after = shifted(both[..., :16], "gz", GZ, -1)
    signs = 1.0 - 2.0 * sign_bits.astype(f32)
    sent = jnp.concatenate([both.reshape(8, 8, 128), tail_of(before, after), signs], axis=0)
    mid = to_all(sent, "gx", GX)
    shared = mid[:, :10]
    sides = [shifted(shared, GY, 16, by) for by in (2, 1, -1, -2)]
    table, weights = prepared_tables(freq_x, freq_y, freq_z, gx, gy, gz)
    at = jnp.stack([gx, gy, gz]).astype(jnp.int32)
    part, kept, ka, kb = run_basis(at, mid, sides, table, weights)
    rows = reduced(part)
    return tuple(run_finish(rows, kept, ka, kb))


def reduced(part):
    pieces = part.reshape(17, GZ, 32).transpose(1, 0, 2).reshape(GZ, 544)
    pieces = lax.all_to_all(pieces, "gz", 0, 0, tiled=True).sum(axis=0)
    pieces = to_all(pieces, GY, 16).sum(axis=0)
    pieces = to_all(pieces, ("gx", "gz"), GX * GZ)
    return pieces.reshape(8, 8, 17, 32).transpose(2, 0, 1, 3).reshape(17, 8, 256)


def solution(mesh):
    split = Mesh(
        mesh.devices.reshape(mesh.shape["gx"], 8, 2, mesh.shape["gz"]), ("gx", "gy_0", "gy_1", "gz")
    )
    return jax.shard_map(
        shards,
        mesh=split,
        in_specs=(P("gx", GY, "gz"), P("gx", GY, "gz"), P("gx", GY, "gz"), P(), P(), P()),
        out_specs=(P("gx", GY, "gz"), P("gx", GY, "gz")),
        check_vma=False,
    )
```

time: 171 us -> 156 us (0.912)
  Pallas kernels: 56.9 us -> 35 us
  waiting for transfers between devices: 17.8 us -> 21.3 us
  local copies, waits for them, and re-layouts: 6.11 us -> 8.25 us
  starting transfers between devices: 35.9 us -> 34 us
  blocking collectives: 47.1 us -> 48.9 us
    pallas_call x1, Pallas kernels: 41.3 us -> 25.2 us  [run_basis(): pl.pallas_call(basis_kernel, out_shape=[jax.ShapeDtypeStruct((DEGREE + 1,...]
    pallas_call x1, Pallas kernels: 15.6 us -> 9.74 us  [run_finish(): pl.pallas_call(finish_kernel, out_shape=[jax.ShapeDtypeStruct((4, 8, 128)...]
    all_to_all x1, waiting for transfers between devices: 9.53 us -> 13.5 us  [to_all(): lax.all_to_all(jnp.broadcast_to(value[None], (size, *value.shape)), axis,...]
    unnamed x11 -> x5, local copies, waits for them, and re-layouts: 0.72 us -> 4.27 us
    unnamed x0 -> x5, other arithmetic: none -> 2.84 us
    ppermute x6, starting transfers between devices: 19.5 us -> 17.6 us  [shifted(): return lax.ppermute(value, axis_name, pairs)]
    all_to_all x1, blocking collectives: 13.8 us -> 15.6 us  [reduced(): pieces = lax.all_to_all(pieces, 'gz', 0, 0, tiled=True).sum(axis=0)]
  transfers between devices with their start and end apart: 7 -> 7, of which waited for: 3 -> 3; matrix products, arithmetic and copies ran while one was open for 4% -> 5% of each run, Pallas kernels for 0% -> 0%
where the time goes in v2:
time: 156 us; the launch traced here: 155 us
  blocking collectives  48.9 us (31%)
  Pallas kernels  35 us (22%)
  starting transfers between devices  34 us (22%)
  waiting for transfers between devices  21.3 us (14%)
  local copies, waits for them, and re-layouts  8.25 us (5%)
  other arithmetic  6.65 us (4%)
    all_to_all x2, blocking collectives, to_all(): lax.all_to_all(jnp.broadcast_to(value[None], (size, *value.shape)), axis,...  33.3 us
    pallas_call x1, Pallas kernels, run_basis(): pl.pallas_call(basis_kernel, out_shape=[jax.ShapeDtypeStruct((DEGREE + 1,...  25.2 us
    ppermute x6, starting transfers between devices, shifted(): return lax.ppermute(value, axis_name, pairs)  17.6 us
    all_to_all x1, starting transfers between devices, to_all(): lax.all_to_all(jnp.broadcast_to(value[None], (size, *value.shape)), axis,...  16.4 us
    all_to_all x1, blocking collectives, reduced(): pieces = lax.all_to_all(pieces, 'gz', 0, 0, tiled=True).sum(axis=0)  15.6 us
    all_to_all x1, waiting for transfers between devices, to_all(): lax.all_to_all(jnp.broadcast_to(value[None], (size, *value.shape)), axis,...  13.5 us
    pallas_call x1, Pallas kernels, run_finish(): pl.pallas_call(finish_kernel, out_shape=[jax.ShapeDtypeStruct((4, 8, 128)...  9.74 us
    ppermute x6, waiting for transfers between devices, shifted(): return lax.ppermute(value, axis_name, pairs)  7.77 us
  transfers between devices with their start and end apart: 7, of which 3 were waited for; matrix products, arithmetic and copies ran while one was open for 5% of the time, Pallas kernels for 0%

profile of v2, /device:TPU:1, one launch (start us, length us, event | category | flops | bytes accessed | tf_op | source)
XLA Modules:
  0.0 154.9 jit_solution(847054969117188109)
XLA Ops:
  0.6 0.9 fusion.10
  1.5 4.1 %collective-permute-start = (f32[2,4,8,16]{3,2,0,1:T(8,128)S(1)}, f32[2,4,8,16]{3,2,0,1:T(8,128)S(1)}, u32[]{:S(2)}, u32[]{:S(2)}) collective-permute-start(f32[2,4,8,16]{3,2,0,1:T(8,128)S(1)} %copy.41), channel_id=1, source_target_pairs={{0,1},{1,2},{2,3},{3,4},{4,5},{5,6},{6,7},{8,9},{9,10},{10,11},{11... | collective-permute-start | bytes 12296 | tf_op jit(solution)/shard_map/ppermute | solution.py:22
  5.6 1.3 collective-permute-start.1
  7.0 0.7 pad_maximum_fusion.1
  7.7 0.8 dynamic_slice.9
  8.5 0.8 dynamic_slice.10
  9.2 0.7 multiply_subtract_fusion
  9.9 0.6 convert_dynamic-update-slice_fusion.1
  10.5 0.6 convert_dynamic-update-slice_fusion
  11.1 0.6 fusion.7
  11.7 0.2 fusion.14
  11.9 0.8 dynamic_slice.11
  12.8 0.8 broadcast_in_dim.6
  13.6 16.4 %all-to-all-start = ((f32[8,14,8,128]{3,2,1,0:T(8,128)}), f32[8,14,8,128]{3,2,1,0:T(8,128)S(1)}, u32[]{:S(2)}, u32[]{:S(2)}) async-start(f32[8,14,8,128]{3,2,1,0:T(8,128)} %broadcast_in_dim.6), calls=%async_computation | async-start | bytes 917504 | tf_op jit(solution)/shard_map/all_to_all | solution.py:332
  30.1 0.6 fusion.8
  30.7 0.6 fusion.6
  31.3 0.6 convert_dynamic-update-slice_fusion.2.table_ref
  31.8 13.5 %all-to-all-done.mid_ref = f32[8,14,8,128]{3,2,1,0:T(8,128)S(1)} async-done(((f32[8,14,8,128]{3,2,1,0:T(8,128)}), f32[8,14,8,128]{3,2,1,0:T(8,128)S(1)}, u32[]{:S(2)}, u32[]{:S(2)}) %all-to-all-start) | async-done | bytes 458784 | tf_op jit(solution)/shard_map/all_to_all | solution.py:332
  45.4 1.3 collective-permute-start.5
  46.7 3.6 %collective-permute-start.4 = (f32[8,10,8,128]{3,2,1,0:T(8,128)S(1)}, f32[8,10,8,128]{3,2,1,0:T(8,128)S(1)}, u32[]{:S(2)}, u32[]{:S(2)}) collective-permute-start(f32[8,10,8,128]{3,2,1,0:T(8,128)S(1)} %slice.56), channel_id=1, source_target_pairs={{8,0},{16,8},{24,16},{32,24},{40,32},{48,40},{56,48},{64,56},{72,6... | collective-permute-start | bytes 983048 | tf_op jit(solution)/shard_map/ppermute | solution.py:22
  50.3 4.2 %collective-permute-start.3 = (f32[8,10,8,128]{3,2,1,0:T(8,128)S(1)}, f32[8,10,8,128]{3,2,1,0:T(8,128)S(1)}, u32[]{:S(2)}, u32[]{:S(2)}) collective-permute-start(f32[8,10,8,128]{3,2,1,0:T(8,128)S(1)} %slice.56), channel_id=1, source_target_pairs={{0,8},{8,16},{16,24},{24,32},{32,40},{40,48},{48,56},{56,64},{64,7... | collective-permute-start | bytes 983048 | tf_op jit(solution)/shard_map/ppermute | solution.py:22
  54.4 3.1 %collective-permute-start.2 = (f32[8,10,8,128]{3,2,1,0:T(8,128)S(1)}, f32[8,10,8,128]{3,2,1,0:T(8,128)S(1)}, u32[]{:S(2)}, u32[]{:S(2)}) collective-permute-start(f32[8,10,8,128]{3,2,1,0:T(8,128)S(1)} %slice.56), channel_id=1, source_target_pairs={{0,16},{8,24},{16,32},{24,40},{32,48},{40,56},{48,64},{56,72},{64,... | collective-permute-start | bytes 983048 | tf_op jit(solution)/shard_map/ppermute | solution.py:22
  57.7 2.5 %collective-permute-done.4.yp1_ref = f32[8,10,8,128]{3,2,1,0:T(8,128)S(1)} collective-permute-done((f32[8,10,8,128]{3,2,1,0:T(8,128)S(1)}, f32[8,10,8,128]{3,2,1,0:T(8,128)S(1)}, u32[]{:S(2)}, u32[]{:S(2)}) %collective-permute-start.4) | collective-permute-done | bytes 327712 | tf_op jit(solution)/shard_map/ppermute | solution.py:22
  60.2 5.2 %collective-permute-done.2.ym2_ref = f32[8,10,8,128]{3,2,1,0:T(8,128)S(1)} collective-permute-done((f32[8,10,8,128]{3,2,1,0:T(8,128)S(1)}, f32[8,10,8,128]{3,2,1,0:T(8,128)S(1)}, u32[]{:S(2)}, u32[]{:S(2)}) %collective-permute-start.2) | collective-permute-done | bytes 327712 | tf_op jit(solution)/shard_map/ppermute | solution.py:22
  65.5 25.2 %basis.1 = (f32[17,256]{1,0:T(8,128)S(1)}, f32[9,20,2,24,128]{4,3,2,1,0:T(8,128)S(1)}, f32[20,2,24,128]{3,2,1,0:T(8,128)S(1)}, f32[20,2,24,128]{3,2,1,0:T(8,128)S(1)}) custom-call(s32[3]{0:T(128)S(1)} %pad_add_fusion.at_ref, f32[8,14,8,128]{3,2,1,0:T(8,128)S(1)} %all-to-all-done.mid_ref, f32[8,10,8,128]{3,2,1,0:T(8,128)S(1)} %collective-permute-done.2.ym2_ref, ...), custom_call_target="tpu_custom_call" | custom-call | tf_op jit(solution)/shard_map/basis/pallas_call | solution.py:284
  90.7 2.0 %copy-done = f32[9,20,2,24,128]{4,3,2,1,0:T(8,128)} copy-done((f32[9,20,2,24,128]{4,3,2,1,0:T(8,128)}, f32[9,20,2,24,128]{4,3,2,1,0:T(8,128)S(1)}, u32[]{:S(2)}) %copy-start) | copy-done | bytes 4423704
  92.9 15.6 %all_to_all.27 = f32[8,1,544]{2,1,0:T(1,128)S(1)} all-to-all(f32[8,1,544]{2,1,0:T(1,128)S(1)} %all_to_all.22), channel_id=1, replica_groups=mesh['gx'=8,'gy_0'=8,'gy_1'=2,'gz'=8] {'gz'}, dimensions={0} | all-to-all | bytes 34816 | tf_op jit(solution)/shard_map/all_to_all | solution.py:363
  108.6 17.5 %all_to_all.28 = f32[16,1,544]{2,1,0:T(1,128)S(1)} all-to-all(f32[16,1,544]{2,1,0:T(1,128)S(1)} %broadcast_in_dim.7), channel_id=1, replica_groups=mesh['gx'=8,'gy_0'=8,'gy_1'=2,'gz'=8] {'gy_0','gy_1'}, dimensions={0} | all-to-all | bytes 69632 | tf_op jit(solution)/shard_map/all_to_all | solution.py:332
  126.2 15.8 %all_to_all.29 = f32[64,1,544]{2,1,0:T(1,128)S(1)} all-to-all(f32[64,1,544]{2,1,0:T(1,128)S(1)} %broadcast_in_dim.8), channel_id=1, replica_groups=mesh['gx'=8,'gy_0'=8,'gy_1'=2,'gz'=8] {'gx','gz'}, dimensions={0} | all-to-all | bytes 278528 | tf_op jit(solution)/shard_map/all_to_all | solution.py:332
  142.0 0.4 reduce.2
  142.9 2.2 %copy-done.1 = f32[9,20,2,24,128]{4,3,2,1,0:T(8,128)S(1)} copy-done((f32[9,20,2,24,128]{4,3,2,1,0:T(8,128)S(1)}, f32[9,20,2,24,128]{4,3,2,1,0:T(8,128)}, u32[]{:S(2)}) %copy-start.1) | copy-done | bytes 4423704
  145.2 9.7 %finish.1 = (f32[4,8,128]{2,1,0:T(8,128)}, f32[4,8,128]{2,1,0:T(8,128)}) custom-call(f32[17,8,256]{2,1,0:T(8,128)S(1)} %reshape.146.rows_ref, f32[9,20,2,24,128]{4,3,2,1,0:T(8,128)S(1)} %copy-done.1, f32[20,2,24,128]{3,2,1,0:T(8,128)S(1)} %get-tuple-element.8.ka_ref, f32[20,2,24,128]{3,2,1,0:T(8,128)S(1)} %get-tuple-element.9.kb_ref), custom_call_target="tpu_custom_call" | custom-call | tf_op jit(solution)/shard_map/finish/pallas_call | solution.py:308
  (28 shorter events, 1.3 us)
Async XLA Ops:
  1.5 11.2 %collective-permute-start = (f32[2,4,8,16]{3,2,0,1:T(8,128)S(1)}, f32[2,4,8,16]{3,2,0,1:T(8,128)S(1)}, u32[]{:S(2)}, u32[]{:S(2)}) collective-permute-start(f32[2,4,8,16]{3,2,0,1:T(8,128)S(1)} %copy.41), channel_id=1, source_target_pairs={{0,1},{1,2},{2,3},{3,4},{4,5},{5,6},{6,7},{8,9},{9,10},{10,11},{11... | collective-permute-start | bytes 12296 | tf_op jit(solution)/shard_map/ppermute | solution.py:22
  5.6 7.0 %collective-permute-start.1 = (f32[2,4,8,16]{3,2,1,0:T(8,128)S(1)}, f32[2,4,8,16]{3,2,1,0:T(8,128)S(1)}, u32[]{:S(2)}, u32[]{:S(2)}) collective-permute-start(f32[2,4,8,16]{3,2,1,0:T(8,128)S(1)} %get-tuple-element.18), channel_id=1, source_target_pairs={{1,0},{2,1},{3,2},{4,3},{5,4},{6,5},{7,6},{9,8},{10,9},{11,10},{12... | collective-permute-start | bytes 12296 | tf_op jit(solution)/shard_map/ppermute | solution.py:22
  13.6 31.8 %all-to-all-start = ((f32[8,14,8,128]{3,2,1,0:T(8,128)}), f32[8,14,8,128]{3,2,1,0:T(8,128)S(1)}, u32[]{:S(2)}, u32[]{:S(2)}) async-start(f32[8,14,8,128]{3,2,1,0:T(8,128)} %broadcast_in_dim.6), calls=%async_computation | async-start | bytes 917504 | tf_op jit(solution)/shard_map/all_to_all | solution.py:332
  45.4 12.3 %collective-permute-start.5 = (f32[8,10,8,128]{3,2,1,0:T(8,128)S(1)}, f32[8,10,8,128]{3,2,1,0:T(8,128)S(1)}, u32[]{:S(2)}, u32[]{:S(2)}) collective-permute-start(f32[8,10,8,128]{3,2,1,0:T(8,128)S(1)} %slice.56), channel_id=1, source_target_pairs={{16,0},{24,8},{32,16},{40,24},{48,32},{56,40},{64,48},{72,56},{80,... | collective-permute-start | bytes 983048 | tf_op jit(solution)/shard_map/ppermute | solution.py:22
  46.7 13.5 %collective-permute-start.4 = (f32[8,10,8,128]{3,2,1,0:T(8,128)S(1)}, f32[8,10,8,128]{3,2,1,0:T(8,128)S(1)}, u32[]{:S(2)}, u32[]{:S(2)}) collective-permute-start(f32[8,10,8,128]{3,2,1,0:T(8,128)S(1)} %slice.56), channel_id=1, source_target_pairs={{8,0},{16,8},{24,16},{32,24},{40,32},{48,40},{56,48},{64,56},{72,6... | collective-permute-start | bytes 983048 | tf_op jit(solution)/shard_map/ppermute | solution.py:22
  50.3 10.0 %collective-permute-start.3 = (f32[8,10,8,128]{3,2,1,0:T(8,128)S(1)}, f32[8,10,8,128]{3,2,1,0:T(8,128)S(1)}, u32[]{:S(2)}, u32[]{:S(2)}) collective-permute-start(f32[8,10,8,128]{3,2,1,0:T(8,128)S(1)} %slice.56), channel_id=1, source_target_pairs={{0,8},{8,16},{16,24},{24,32},{32,40},{40,48},{48,56},{56,64},{64,7... | collective-permute-start | bytes 983048 | tf_op jit(solution)/shard_map/ppermute | solution.py:22
  54.4 11.0 %collective-permute-start.2 = (f32[8,10,8,128]{3,2,1,0:T(8,128)S(1)}, f32[8,10,8,128]{3,2,1,0:T(8,128)S(1)}, u32[]{:S(2)}, u32[]{:S(2)}) collective-permute-start(f32[8,10,8,128]{3,2,1,0:T(8,128)S(1)} %slice.56), channel_id=1, source_target_pairs={{0,16},{8,24},{16,32},{24,40},{32,48},{40,56},{48,64},{56,72},{64,... | collective-permute-start | bytes 983048 | tf_op jit(solution)/shard_map/ppermute | solution.py:22
  90.7 2.0 %copy-start = (f32[9,20,2,24,128]{4,3,2,1,0:T(8,128)}, f32[9,20,2,24,128]{4,3,2,1,0:T(8,128)S(1)}, u32[]{:S(2)}) copy-start(f32[9,20,2,24,128]{4,3,2,1,0:T(8,128)S(1)} %get-tuple-element.7.kept_ref) | copy-start | bytes 13271044
  142.9 2.3 %copy-start.1 = (f32[9,20,2,24,128]{4,3,2,1,0:T(8,128)S(1)}, f32[9,20,2,24,128]{4,3,2,1,0:T(8,128)}, u32[]{:S(2)}) copy-start(f32[9,20,2,24,128]{4,3,2,1,0:T(8,128)} %copy-done) | copy-start | bytes 13271044

commit v3 on v2

--- a/solution.py
+++ b/solution.py
@@ -46,17 +46,19 @@
     ]
 
 
-def next_plane(now, other, coef, scale, x, rows, first, at=None):
+def halves_of(field, x, rows):
+    return [field[x + 1, h, rows[0]:rows[1], :] for h in range(2)]
+
+
+def next_plane(now, other, coef, scale, x, rows, first, sides):
     low, high = rows
-    at = x if at is None else at
-    here = [now[x + 1, h, low:high, :] for h in range(2)]
-    sides = beside_z(here)
+    here = halves_of(now, x, rows)
     out = []
     for h in range(2):
         total = now[x, h, low:high, :] + now[x + 2, h, low:high, :]
         total = total + (now[x + 1, h, low - 1:high - 1, :] + now[x + 1, h, low + 1:high + 1, :])
         total = total + sides[h]
-        value = coef[at, h, low - 8:high - 8, :] * here[h] - scale(h) * total
+        value = coef[x, h, low - 8:high - 8, :] * here[h] - scale(h) * total
         value = 0.5 * value if first else value - other[x + 1, h, low:high, :]
         other[x + 1, h, low:high, :] = value
         out.append(value)
@@ -76,6 +78,8 @@
     lane8 = lax.broadcasted_iota(jnp.int32, (8, 128), 1)
     tail_used = (lane8 < 16) | (lane8 >= 112)
     empty = jnp.zeros((8, 128), f32)
+    for m in range(DEGREE + 1, 3 * GZ):
+        part_ref[m // 3, m % 3:m % 3 + 1, :] = jnp.zeros((1, SHARE), f32)
     for ref in (even, odd):
         for plane in (0, NX + 1):
             for h in range(2):
@@ -99,12 +103,13 @@
                 coef[x, 1, rows, :] = (tail - 1.0) * mask[1, rows, :]
         return carry
 
-    lax.fori_loop(0, GX, fill, 0)
+    for chip in range(GX):
+        fill(chip, 0)
 
     def put(m, chip, k, first, second):
         block = jnp.concatenate([first * mid_ref[chip, 10 + k], second * mid_ref[chip, 11 + k]], axis=0)
         high, middle, low = split_3(block)
-        rows = pl.ds(pl.multiple_of(256 * (m % 2) + 32 * chip + 8 * k, 16), 16)
+        rows = slice(256 * (m % 4) + 32 * chip + 8 * k, 256 * (m % 4) + 32 * chip + 8 * k + 16)
         lhs[rows, 0:128] = middle
         lhs[rows, 128:256] = high
         lhs[rows, 256:384] = low
@@ -116,14 +121,15 @@
         total = jnp.dot(stacked, table_ref[...], preferred_element_type=f32)
         for m in range(begin, end):
             own = total[256 * (m - begin):256 * (m - begin + 1)]
-            part_ref[m:m + 1, :] = jnp.sum(own * w_ref[...], axis=0, keepdims=True)
+            part_ref[m // 3, m % 3:m % 3 + 1, :] = jnp.sum(own * w_ref[...], axis=0, keepdims=True)
 
     def keep(m, ref):
         def one(p, carry):
             plane = jnp.clip(4 * gx - 7 + p, 0, NX + 1)
             kept_ref[m, p] = ref[plane, :, 16:40, :]
             return carry
-        lax.fori_loop(0, 20, one, 0, unroll=4)
+        for p in range(20):
+            one(p, 0)
 
     def keep_coef(p, carry):
         x = 4 * gx - 8 + p
@@ -132,33 +138,26 @@
         kb_ref[p] = mask[:, 8:32, :] * real
         return carry
 
-    lax.fori_loop(0, 20, keep_coef, 0)
-
-    def first_put(chip, carry):
-        for k in (0, 2):
-            put(0, chip, k, *[even[4 * chip + k + d + 1, 0, 24:32, :] for d in range(2)])
-        return carry
-
-    lax.fori_loop(0, GX, first_put, 0)
+    for p in range(20):
+        keep_coef(p, 0)
+
+    for x in range(0, NX, 2):
+        put(0, x // 4, x % 4, even[x + 1, 0, 24:32, :], even[x + 2, 0, 24:32, :])
     keep(0, even)
     now, other = even, odd
     for m in range(1, DEGREE + 1):
         rows = (8, 48) if m <= BASIS else (16, 40)
-
-        def step(chip, carry, m=m, rows=rows, now=now, other=other):
-            own = slice(24 - rows[0], 32 - rows[0])
-            for k in (0, 2):
-                pair = []
-                for d in range(2):
-                    x = 4 * chip + k + d
-                    scale = lambda h: mask[h, rows[0] - 8:rows[1] - 8, :]
-                    pair.append(next_plane(now, other, coef, scale, x, rows, m == 1)[0][own])
-                put(m, chip, k, *pair)
-            return carry
-
-        lax.fori_loop(0, GX, step, 0)
-        if m % 2:
-            project(m - 1, m + 1)
+        cut = slice(rows[0] - 8, rows[1] - 8)
+        own = slice(24 - rows[0], 32 - rows[0])
+        scale = lambda h: mask[h, cut, :]
+        for x in range(0, NX, 2):
+            pair = []
+            for d in range(2):
+                beside = beside_z(halves_of(now, x + d, rows))
+                pair.append(next_plane(now, other, coef, scale, x + d, rows, m == 1, beside)[0][own])
+            put(m, x // 4, x % 4, *pair)
+        if m % 4 == 3:
+            project(m - 3, m + 1)
         if m <= BASIS:
             keep(m, other)
         now, other = other, now
@@ -187,6 +186,7 @@
     basis, upper, overlap, inverse = [], {}, {}, []
     for j in range(BASIS):
         column = columns[j]
+        square = dot_of(column, column)
         if j:
             seen = [dot_of(basis[i], column) for i in range(j)]
             amounts = []
@@ -198,14 +198,18 @@
             for i in range(j):
                 column = column - amounts[i] * basis[i]
                 upper[i, j] = upper[i, j] + amounts[i]
-        length = jnp.sqrt(dot_of(column, column) + tiny_value)
+                spread = overlap[i, i] * amounts[i] - 2.0 * seen[i]
+                for k in range(i):
+                    spread = spread + (2.0 * overlap[i, k]) * amounts[k]
+                square = square + spread * amounts[i]
+        length = jnp.sqrt(jnp.maximum(square, 0.0) + tiny_value)
         inverse.append(1.0 / length)
         basis.append(column * inverse[j])
         for later in range(j + 1, BASIS):
             amount = dot_of(basis[j], columns[later])
             columns[later] = columns[later] - amount * basis[j]
             upper[j, later] = amount
-        for k in range(j):
+        for k in range(j + 1):
             overlap[j, k] = dot_of(basis[j], basis[k])
     solved = [dot_of(vector, target) for vector in basis]
     for i in range(BASIS - 1, -1, -1):
@@ -226,65 +230,60 @@
 
 
 def finish_kernel(rows_ref, kept_ref, ka_ref, kb_ref, sol_ref, res_ref, even, odd):
-    rows = [rows_ref[m] for m in range(DEGREE + 1)]
+    rows = []
+    for m in range(DEGREE + 1):
+        rows.append(jnp.concatenate(
+            [rows_ref[GZ * chip + m // 3, m % 3:m % 3 + 1, :] for chip in range(GX)], axis=0
+        ))
+    for ref in (even, odd):
+        for p in range(1, 21):
+            for h in range(2):
+                ref[p, h, 0:8, :] = jnp.zeros((8, 128), f32)
+                ref[p, h, 32:40, :] = jnp.zeros((8, 128), f32)
     first = solve(images_of(rows[:BASIS + 1]), rows[0])
     rest = remainder_of(first)
+    for p in range(20):
+        for h in range(2):
+            value = rest[0] * kept_ref[0, p, h]
+            for m in range(1, BASIS + 1):
+                value = value + rest[m] * kept_ref[m, p, h]
+            even[p + 1, h, 8:32, :] = value
     turned = []
     for j in range(BASIS + 1):
         value = rest[0] * rows[j]
         for m in range(1, BASIS + 1):
             value = value + (0.5 * rest[m]) * (rows[m + j] + rows[abs(m - j)])
         turned.append(value)
+    fields = [[even[9 + p, 0, 16:24, :] for p in range(4)]]
+    now, other = even, odd
+    for m in range(1, BASIS + 1):
+        fields.append([])
+        for p in range(m, 20 - m):
+            sides = beside_z(halves_of(now, p, (8, 32)))
+            value = next_plane(now, other, ka_ref, lambda h: kb_ref[p, h], p, (8, 32), m == 1, sides)
+            if 8 <= p < 12:
+                fields[m].append(value[0][8:16])
+        now, other = other, now
     second = solve(images_of(turned), turned[0])
     last = remainder_of(second)
-
-    for ref in (even, odd):
-        for h in range(2):
-            ref[0, h] = jnp.zeros((40, 128), f32)
-            ref[21, h] = jnp.zeros((40, 128), f32)
-
-    def start(p, carry):
-        for h in range(2):
-            value = rest[0] * kept_ref[0, p, h]
-            for m in range(1, BASIS + 1):
-                value = value + rest[m] * kept_ref[m, p, h]
-            even[p + 1, h, 8:32, :] = value
-            for ref in (even, odd):
-                ref[p + 1, h, 0:8, :] = jnp.zeros((8, 128), f32)
-                ref[p + 1, h, 32:40, :] = jnp.zeros((8, 128), f32)
-        return carry
-
-    lax.fori_loop(0, 20, start, 0)
     for p in range(4):
         value = first[0] * kept_ref[0, 8 + p, 0, 8:16, :]
         for m in range(1, BASIS):
             value = value + first[m] * kept_ref[m, 8 + p, 0, 8:16, :]
-        here = even[9 + p, 0, 16:24, :]
-        sol_ref[p] = value + second[0] * here
-        res_ref[p] = last[0] * here
-    now, other = even, odd
-    for m in range(1, BASIS + 1):
-        def step(q, carry, m=m, now=now, other=other):
-            for d in range(2):
-                p = m + 2 * q + d
-                scale = lambda h: kb_ref[p, h]
-                next_plane(now, other, ka_ref, scale, p, (8, 32), m == 1)
-            return carry
-
-        lax.fori_loop(0, 10 - m, step, 0)
-        for p in range(4):
-            here = other[9 + p, 0, 16:24, :]
-            if m < BASIS:
-                sol_ref[p] += second[m] * here
-            res_ref[p] += last[m] * here
-        now, other = other, now
+        for m in range(BASIS):
+            value = value + second[m] * fields[m][p]
+        sol_ref[p] = value
+        value = last[0] * fields[0][p]
+        for m in range(1, BASIS + 1):
+            value = value + last[m] * fields[m][p]
+        res_ref[p] = value
 
 
 def run_basis(at, mid, sides, table, weights, interpret=False):
     return pl.pallas_call(
         basis_kernel,
         out_shape=[
-            jax.ShapeDtypeStruct((DEGREE + 1, SHARE), f32),
+            jax.ShapeDtypeStruct((GZ, 3, SHARE), f32),
             jax.ShapeDtypeStruct((BASIS + 1, 20, 2, 24, 128), f32),
             jax.ShapeDtypeStruct((20, 2, 24, 128), f32),
             jax.ShapeDtypeStruct((20, 2, 24, 128), f32),
@@ -296,7 +295,7 @@
             VMEM((NX + 2, 2, 56, 128), f32),
             VMEM((NX, 2, 40, 128), f32),
             VMEM((2, 40, 128), f32),
-            VMEM((512, 384), bf16),
+            VMEM((1024, 384), bf16),
         ],
         compiler_params=pltpu.CompilerParams(vmem_limit_bytes=28 << 20),
         name="basis",
@@ -351,6 +350,7 @@
     mid = to_all(sent, "gx", GX)
     shared = mid[:, :10]
     sides = [shifted(shared, GY, 16, by) for by in (2, 1, -1, -2)]
+    freq_x, freq_y, freq_z, mid = lax.optimization_barrier((freq_x, freq_y, freq_z, mid))
     table, weights = prepared_tables(freq_x, freq_y, freq_z, gx, gy, gz)
     at = jnp.stack([gx, gy, gz]).astype(jnp.int32)
     part, kept, ka, kb = run_basis(at, mid, sides, table, weights)
@@ -359,11 +359,9 @@
 
 
 def reduced(part):
-    pieces = part.reshape(17, GZ, 32).transpose(1, 0, 2).reshape(GZ, 544)
-    pieces = lax.all_to_all(pieces, "gz", 0, 0, tiled=True).sum(axis=0)
+    pieces = lax.all_to_all(part, "gz", 0, 0, tiled=True).sum(axis=0)
     pieces = to_all(pieces, GY, 16).sum(axis=0)
-    pieces = to_all(pieces, ("gx", "gz"), GX * GZ)
-    return pieces.reshape(8, 8, 17, 32).transpose(2, 0, 1, 3).reshape(17, 8, 256)
+    return to_all(pieces, ("gx", "gz"), GX * GZ)
 
 
 def solution(mesh):

time: 156 us -> 134 us (0.86)
  Pallas kernels: 35 us -> 16.4 us
  waiting for transfers between devices: 21.3 us -> 17 us
  starting transfers between devices: 34 us -> 35.9 us
    pallas_call x1, Pallas kernels: 25.2 us -> 11.4 us  [run_basis(): pl.pallas_call(basis_kernel, out_shape=[jax.ShapeDtypeStruct((GZ, 3, SHAR...]
    pallas_call x1, Pallas kernels: 9.74 us -> 5 us  [run_finish(): pl.pallas_call(finish_kernel, out_shape=[jax.ShapeDtypeStruct((4, 8, 128)...]
    ppermute x6, waiting for transfers between devices: 7.77 us -> 3.64 us  [shifted(): return lax.ppermute(value, axis_name, pairs)]
    all_to_all x2, blocking collectives: 33.3 us -> 35.3 us  [to_all(): lax.all_to_all(jnp.broadcast_to(value[None], (size, *value.shape)), axis,...]
    ppermute x6, starting transfers between devices: 17.6 us -> 19.5 us  [shifted(): return lax.ppermute(value, axis_name, pairs)]
    all_to_all x1, blocking collectives: 15.6 us -> 14 us  [reduced(): pieces = lax.all_to_all(part, 'gz', 0, 0, tiled=True).sum(axis=0)]
  transfers between devices with their start and end apart: 7 -> 7, of which waited for: 3 -> 3; matrix products, arithmetic and copies ran while one was open for 5% -> 6% of each run, Pallas kernels for 0% -> 0%
where the time goes in v3:
time: 134 us; the launch traced here: 133 us
  blocking collectives  49.2 us (37%)
  starting transfers between devices  35.9 us (27%)
  waiting for transfers between devices  17 us (13%)
  Pallas kernels  16.4 us (12%)
  local copies, waits for them, and re-layouts  7.51 us (6%)
  other arithmetic  6.26 us (5%)
    all_to_all x2, blocking collectives, to_all(): lax.all_to_all(jnp.broadcast_to(value[None], (size, *value.shape)), axis,...  35.3 us
    ppermute x6, starting transfers between devices, shifted(): return lax.ppermute(value, axis_name, pairs)  19.5 us
    all_to_all x1, starting transfers between devices, to_all(): lax.all_to_all(jnp.broadcast_to(value[None], (size, *value.shape)), axis,...  16.4 us
    all_to_all x1, blocking collectives, reduced(): pieces = lax.all_to_all(part, 'gz', 0, 0, tiled=True).sum(axis=0)  14 us
    all_to_all x1, waiting for transfers between devices, to_all(): lax.all_to_all(jnp.broadcast_to(value[None], (size, *value.shape)), axis,...  13.4 us
    pallas_call x1, Pallas kernels, run_basis(): pl.pallas_call(basis_kernel, out_shape=[jax.ShapeDtypeStruct((GZ, 3, SHAR...  11.4 us
    pallas_call x1, Pallas kernels, run_finish(): pl.pallas_call(finish_kernel, out_shape=[jax.ShapeDtypeStruct((4, 8, 128)...  5 us
    unnamed x5, local copies, waits for them, and re-layouts  4.26 us
  transfers between devices with their start and end apart: 7, of which 3 were waited for; matrix products, arithmetic and copies ran while one was open for 6% of the time, Pallas kernels for 0%

profile of v3, /device:TPU:1, one launch (start us, length us, event | category | flops | bytes accessed | tf_op | source)
XLA Modules:
  0.0 133.1 jit_solution(16239495766628720102)
XLA Ops:
  0.6 0.9 fusion.10
  1.5 4.1 %collective-permute-start = (f32[2,4,8,16]{3,2,0,1:T(8,128)S(1)}, f32[2,4,8,16]{3,2,0,1:T(8,128)S(1)}, u32[]{:S(2)}, u32[]{:S(2)}) collective-permute-start(f32[2,4,8,16]{3,2,0,1:T(8,128)S(1)} %copy.22), channel_id=1, source_target_pairs={{0,1},{1,2},{2,3},{3,4},{4,5},{5,6},{6,7},{8,9},{9,10},{10,11},{11... | collective-permute-start | bytes 12296 | tf_op jit(solution)/shard_map/ppermute | solution.py:22
  5.6 1.3 collective-permute-start.1
  6.9 0.7 multiply_subtract_fusion
  7.7 0.7 pad_maximum_fusion.1
  8.4 1.9 %collective-permute-done.1 = f32[2,4,8,16]{3,2,1,0:T(8,128)S(1)} collective-permute-done((f32[2,4,8,16]{3,2,1,0:T(8,128)S(1)}, f32[2,4,8,16]{3,2,1,0:T(8,128)S(1)}, u32[]{:S(2)}, u32[]{:S(2)}) %collective-permute-start.1) | collective-permute-done | bytes 4128 | tf_op jit(solution)/shard_map/ppermute | solution.py:22
  10.4 0.8 broadcast_in_dim.6
  11.2 16.4 %all-to-all-start = ((f32[8,14,8,128]{3,2,1,0:T(8,128)}), f32[8,14,8,128]{3,2,1,0:T(8,128)S(1)}, u32[]{:S(2)}, u32[]{:S(2)}) async-start(f32[8,14,8,128]{3,2,1,0:T(8,128)} %broadcast_in_dim.6), calls=%async_computation | async-start | bytes 917504 | tf_op jit(solution)/shard_map/all_to_all | solution.py:331
  27.7 13.4 %all-to-all-done.mid_ref = f32[8,14,8,128]{3,2,1,0:T(8,128)S(1)} async-done(((f32[8,14,8,128]{3,2,1,0:T(8,128)}), f32[8,14,8,128]{3,2,1,0:T(8,128)S(1)}, u32[]{:S(2)}, u32[]{:S(2)}) %all-to-all-start) | async-done | bytes 458784 | tf_op jit(solution)/shard_map/all_to_all | solution.py:331
  41.2 1.3 collective-permute-start.5
  42.5 5.4 %collective-permute-start.4 = (f32[8,10,8,128]{3,2,1,0:T(8,128)S(1)}, f32[8,10,8,128]{3,2,1,0:T(8,128)S(1)}, u32[]{:S(2)}, u32[]{:S(2)}) collective-permute-start(f32[8,10,8,128]{3,2,1,0:T(8,128)S(1)} %slice.56), channel_id=1, source_target_pairs={{8,0},{16,8},{24,16},{32,24},{40,32},{48,40},{56,48},{64,56},{72,6... | collective-permute-start | bytes 983048 | tf_op jit(solution)/shard_map/ppermute | solution.py:22
  47.9 4.2 %collective-permute-start.3 = (f32[8,10,8,128]{3,2,1,0:T(8,128)S(1)}, f32[8,10,8,128]{3,2,1,0:T(8,128)S(1)}, u32[]{:S(2)}, u32[]{:S(2)}) collective-permute-start(f32[8,10,8,128]{3,2,1,0:T(8,128)S(1)} %slice.56), channel_id=1, source_target_pairs={{0,8},{8,16},{16,24},{24,32},{32,40},{40,48},{48,56},{56,64},{64,7... | collective-permute-start | bytes 983048 | tf_op jit(solution)/shard_map/ppermute | solution.py:22
  52.1 3.1 %collective-permute-start.2 = (f32[8,10,8,128]{3,2,1,0:T(8,128)S(1)}, f32[8,10,8,128]{3,2,1,0:T(8,128)S(1)}, u32[]{:S(2)}, u32[]{:S(2)}) collective-permute-start(f32[8,10,8,128]{3,2,1,0:T(8,128)S(1)} %slice.56), channel_id=1, source_target_pairs={{0,16},{8,24},{16,32},{24,40},{32,48},{40,56},{48,64},{56,72},{64,... | collective-permute-start | bytes 983048 | tf_op jit(solution)/shard_map/ppermute | solution.py:22
  55.2 0.8 dynamic_slice.9
  56.0 0.8 dynamic_slice.10
  56.7 0.8 dynamic_slice.11
  57.5 0.6 convert_dynamic-update-slice_fusion.1
  58.1 0.6 convert_dynamic-update-slice_fusion
  58.6 0.6 fusion.7
  59.2 0.6 fusion.8
  59.8 0.6 fusion.6
  60.4 0.6 convert_dynamic-update-slice_fusion.2.table_ref
  60.9 0.2 fusion.14
  61.2 0.1 fusion.19
  61.4 1.7 %collective-permute-done.2.ym2_ref = f32[8,10,8,128]{3,2,1,0:T(8,128)S(1)} collective-permute-done((f32[8,10,8,128]{3,2,1,0:T(8,128)S(1)}, f32[8,10,8,128]{3,2,1,0:T(8,128)S(1)}, u32[]{:S(2)}, u32[]{:S(2)}) %collective-permute-start.2) | collective-permute-done | bytes 327712 | tf_op jit(solution)/shard_map/ppermute | solution.py:22
  63.1 11.4 %basis.1 = (f32[8,3,256]{2,1,0:T(4,128)S(1)}, f32[9,20,2,24,128]{4,3,2,1,0:T(8,128)S(1)}, f32[20,2,24,128]{3,2,1,0:T(8,128)S(1)}, f32[20,2,24,128]{3,2,1,0:T(8,128)S(1)}) custom-call(s32[3]{0:T(128)S(1)} %pad_add_fusion.at_ref, f32[8,14,8,128]{3,2,1,0:T(8,128)S(1)} %all-to-all-done.mid_ref, f32[8,10,8,128]{3,2,1,0:T(8,128)S(1)} %collective-permute-done.2.ym2_ref, ...), custom_call_target="tpu_custom_call" | custom-call | tf_op jit(solution)/shard_map/basis/pallas_call | solution.py:283
  74.5 2.0 %copy-done = f32[9,20,2,24,128]{4,3,2,1,0:T(8,128)} copy-done((f32[9,20,2,24,128]{4,3,2,1,0:T(8,128)}, f32[9,20,2,24,128]{4,3,2,1,0:T(8,128)S(1)}, u32[]{:S(2)}) %copy-start) | copy-done | bytes 4423704
  76.5 14.0 %all_to_all.20 = f32[8,3,256]{2,1,0:T(4,128)S(1)} all-to-all(f32[8,3,256]{2,1,0:T(4,128)S(1)} %get-tuple-element.14), channel_id=1, replica_groups=mesh['gx'=8,'gy_0'=8,'gy_1'=2,'gz'=8] {'gz'}, dimensions={0} | all-to-all | bytes 49152 | tf_op jit(solution)/shard_map/all_to_all | solution.py:362
  90.5 17.9 %all_to_all.21 = f32[16,3,256]{2,1,0:T(4,128)S(1)} all-to-all(f32[16,3,256]{2,1,0:T(4,128)S(1)} %broadcast_in_dim.7), channel_id=1, replica_groups=mesh['gx'=8,'gy_0'=8,'gy_1'=2,'gz'=8] {'gy_0','gy_1'}, dimensions={0} | all-to-all | bytes 98304 | tf_op jit(solution)/shard_map/all_to_all | solution.py:331
  108.5 17.4 %all_to_all.22.rows_ref = f32[64,3,256]{2,1,0:T(4,128)S(1)} all-to-all(f32[64,3,256]{2,1,0:T(4,128)S(1)} %broadcast_in_dim.8), channel_id=1, replica_groups=mesh['gx'=8,'gy_0'=8,'gy_1'=2,'gz'=8] {'gx','gz'}, dimensions={0} | all-to-all | bytes 393216 | tf_op jit(solution)/shard_map/all_to_all | solution.py:331
  125.8 2.3 %copy-done.1 = f32[9,20,2,24,128]{4,3,2,1,0:T(8,128)S(1)} copy-done((f32[9,20,2,24,128]{4,3,2,1,0:T(8,128)S(1)}, f32[9,20,2,24,128]{4,3,2,1,0:T(8,128)}, u32[]{:S(2)}) %copy-start.1) | copy-done | bytes 4423704
  128.1 5.0 %finish.1 = (f32[4,8,128]{2,1,0:T(8,128)}, f32[4,8,128]{2,1,0:T(8,128)}) custom-call(f32[64,3,256]{2,1,0:T(4,128)S(1)} %all_to_all.22.rows_ref, f32[9,20,2,24,128]{4,3,2,1,0:T(8,128)S(1)} %copy-done.1, f32[20,2,24,128]{3,2,1,0:T(8,128)S(1)} %get-tuple-element.16.ka_ref, f32[20,2,24,128]{3,2,1,0:T(8,128)S(1)} %get-tuple-element.17.kb_ref), custom_call_target="tpu_custom_call" | custom-call | tf_op jit(solution)/shard_map/finish/pallas_call | solution.py:307
  (21 shorter events, 0.4 us)
Async XLA Ops:
  1.5 6.9 %collective-permute-start = (f32[2,4,8,16]{3,2,0,1:T(8,128)S(1)}, f32[2,4,8,16]{3,2,0,1:T(8,128)S(1)}, u32[]{:S(2)}, u32[]{:S(2)}) collective-permute-start(f32[2,4,8,16]{3,2,0,1:T(8,128)S(1)} %copy.22), channel_id=1, source_target_pairs={{0,1},{1,2},{2,3},{3,4},{4,5},{5,6},{6,7},{8,9},{9,10},{10,11},{11... | collective-permute-start | bytes 12296 | tf_op jit(solution)/shard_map/ppermute | solution.py:22
  5.6 4.7 %collective-permute-start.1 = (f32[2,4,8,16]{3,2,1,0:T(8,128)S(1)}, f32[2,4,8,16]{3,2,1,0:T(8,128)S(1)}, u32[]{:S(2)}, u32[]{:S(2)}) collective-permute-start(f32[2,4,8,16]{3,2,1,0:T(8,128)S(1)} %get-tuple-element.26), channel_id=1, source_target_pairs={{1,0},{2,1},{3,2},{4,3},{5,4},{6,5},{7,6},{9,8},{10,9},{11,10},{12... | collective-permute-start | bytes 12296 | tf_op jit(solution)/shard_map/ppermute | solution.py:22
  11.2 29.9 %all-to-all-start = ((f32[8,14,8,128]{3,2,1,0:T(8,128)}), f32[8,14,8,128]{3,2,1,0:T(8,128)S(1)}, u32[]{:S(2)}, u32[]{:S(2)}) async-start(f32[8,14,8,128]{3,2,1,0:T(8,128)} %broadcast_in_dim.6), calls=%async_computation | async-start | bytes 917504 | tf_op jit(solution)/shard_map/all_to_all | solution.py:331
  41.2 20.2 %collective-permute-start.5 = (f32[8,10,8,128]{3,2,1,0:T(8,128)S(1)}, f32[8,10,8,128]{3,2,1,0:T(8,128)S(1)}, u32[]{:S(2)}, u32[]{:S(2)}) collective-permute-start(f32[8,10,8,128]{3,2,1,0:T(8,128)S(1)} %slice.56), channel_id=1, source_target_pairs={{16,0},{24,8},{32,16},{40,24},{48,32},{56,40},{64,48},{72,56},{80,... | collective-permute-start | bytes 983048 | tf_op jit(solution)/shard_map/ppermute | solution.py:22
  42.5 18.9 %collective-permute-start.4 = (f32[8,10,8,128]{3,2,1,0:T(8,128)S(1)}, f32[8,10,8,128]{3,2,1,0:T(8,128)S(1)}, u32[]{:S(2)}, u32[]{:S(2)}) collective-permute-start(f32[8,10,8,128]{3,2,1,0:T(8,128)S(1)} %slice.56), channel_id=1, source_target_pairs={{8,0},{16,8},{24,16},{32,24},{40,32},{48,40},{56,48},{64,56},{72,6... | collective-permute-start | bytes 983048 | tf_op jit(solution)/shard_map/ppermute | solution.py:22
  47.9 13.4 %collective-permute-start.3 = (f32[8,10,8,128]{3,2,1,0:T(8,128)S(1)}, f32[8,10,8,128]{3,2,1,0:T(8,128)S(1)}, u32[]{:S(2)}, u32[]{:S(2)}) collective-permute-start(f32[8,10,8,128]{3,2,1,0:T(8,128)S(1)} %slice.56), channel_id=1, source_target_pairs={{0,8},{8,16},{16,24},{24,32},{32,40},{40,48},{48,56},{56,64},{64,7... | collective-permute-start | bytes 983048 | tf_op jit(solution)/shard_map/ppermute | solution.py:22
  52.1 11.0 %collective-permute-start.2 = (f32[8,10,8,128]{3,2,1,0:T(8,128)S(1)}, f32[8,10,8,128]{3,2,1,0:T(8,128)S(1)}, u32[]{:S(2)}, u32[]{:S(2)}) collective-permute-start(f32[8,10,8,128]{3,2,1,0:T(8,128)S(1)} %slice.56), channel_id=1, source_target_pairs={{0,16},{8,24},{16,32},{24,40},{32,48},{40,56},{48,64},{56,72},{64,... | collective-permute-start | bytes 983048 | tf_op jit(solution)/shard_map/ppermute | solution.py:22
  74.5 2.0 %copy-start = (f32[9,20,2,24,128]{4,3,2,1,0:T(8,128)}, f32[9,20,2,24,128]{4,3,2,1,0:T(8,128)S(1)}, u32[]{:S(2)}) copy-start(f32[9,20,2,24,128]{4,3,2,1,0:T(8,128)S(1)} %get-tuple-element.15.kept_ref) | copy-start | bytes 13271044
  125.8 2.3 %copy-start.1 = (f32[9,20,2,24,128]{4,3,2,1,0:T(8,128)S(1)}, f32[9,20,2,24,128]{4,3,2,1,0:T(8,128)}, u32[]{:S(2)}) copy-start(f32[9,20,2,24,128]{4,3,2,1,0:T(8,128)} %copy-done) | copy-start | bytes 13271044

commit v4 on v3

--- a/solution.py
+++ b/solution.py
@@ -66,7 +66,7 @@
 
 
 def basis_kernel(at_ref, mid_ref, ym2_ref, ym1_ref, yp1_ref, yp2_ref, table_ref, w_ref,
-                 part_ref, kept_ref, ka_ref, kb_ref, even, odd, coef, mask, lhs):
+                 part_ref, kept_ref, ka_ref, kb_ref, even, odd, coef, mask, lhs, held, held_a, held_b, sems):
     gx, gy, gz = at_ref[0], at_ref[1], at_ref[2]
     row = lax.broadcasted_iota(jnp.int32, (40, 128), 0) - 16 + gy * 8
     lane = lax.broadcasted_iota(jnp.int32, (40, 128), 1)
@@ -126,20 +126,28 @@
     def keep(m, ref):
         def one(p, carry):
             plane = jnp.clip(4 * gx - 7 + p, 0, NX + 1)
-            kept_ref[m, p] = ref[plane, :, 16:40, :]
+            held[m, p] = ref[plane, :, 16:40, :]
             return carry
         for p in range(20):
             one(p, 0)
+        moves.append(pltpu.make_async_copy(held.at[m], kept_ref.at[m], sems.at[m]))
+        moves[-1].start()
 
     def keep_coef(p, carry):
         x = 4 * gx - 8 + p
         real = ((x >= 0) & (x < NX)).astype(f32)
-        ka_ref[p] = coef[jnp.clip(x, 0, NX - 1), :, 8:32, :] * real
-        kb_ref[p] = mask[:, 8:32, :] * real
+        held_a[p] = coef[jnp.clip(x, 0, NX - 1), :, 8:32, :] * real
+        held_b[p] = mask[:, 8:32, :] * real
         return carry
 
     for p in range(20):
         keep_coef(p, 0)
+    moves = [
+        pltpu.make_async_copy(held_a, ka_ref, sems.at[BASIS + 1]),
+        pltpu.make_async_copy(held_b, kb_ref, sems.at[BASIS + 2]),
+    ]
+    for move in moves:
+        move.start()
 
     for x in range(0, NX, 2):
         put(0, x // 4, x % 4, even[x + 1, 0, 24:32, :], even[x + 2, 0, 24:32, :])
@@ -162,6 +170,8 @@
             keep(m, other)
         now, other = other, now
     project(DEGREE, DEGREE + 1)
+    for move in moves:
+        move.wait()
 
 
 def total_of(value):
@@ -229,7 +239,13 @@
     return out
 
 
-def finish_kernel(rows_ref, kept_ref, ka_ref, kb_ref, sol_ref, res_ref, even, odd):
+def finish_kernel(rows_ref, far_ref, far_a, far_b, sol_ref, res_ref, even, odd, kept_ref, ka_ref, kb_ref, sems):
+    moves = [
+        pltpu.make_async_copy(far, near, sems.at[n])
+        for n, (far, near) in enumerate(((far_ref, kept_ref), (far_a, ka_ref), (far_b, kb_ref)))
+    ]
+    for move in moves:
+        move.start()
     rows = []
     for m in range(DEGREE + 1):
         rows.append(jnp.concatenate(
@@ -242,6 +258,8 @@
                 ref[p, h, 32:40, :] = jnp.zeros((8, 128), f32)
     first = solve(images_of(rows[:BASIS + 1]), rows[0])
     rest = remainder_of(first)
+    for move in moves:
+        move.wait()
     for p in range(20):
         for h in range(2):
             value = rest[0] * kept_ref[0, p, h]
@@ -284,18 +302,22 @@
         basis_kernel,
         out_shape=[
             jax.ShapeDtypeStruct((GZ, 3, SHARE), f32),
-            jax.ShapeDtypeStruct((BASIS + 1, 20, 2, 24, 128), f32),
-            jax.ShapeDtypeStruct((20, 2, 24, 128), f32),
-            jax.ShapeDtypeStruct((20, 2, 24, 128), f32),
+            pltpu.HBM((BASIS + 1, 20, 2, 24, 128), f32),
+            pltpu.HBM((20, 2, 24, 128), f32),
+            pltpu.HBM((20, 2, 24, 128), f32),
         ],
         in_specs=[pl.BlockSpec(memory_space=pltpu.SMEM)] + [pl.BlockSpec(memory_space=VMEM)] * 7,
-        out_specs=[pl.BlockSpec(memory_space=VMEM)] * 4,
+        out_specs=[pl.BlockSpec(memory_space=m) for m in (VMEM, pltpu.HBM, pltpu.HBM, pltpu.HBM)],
         scratch_shapes=[
             VMEM((NX + 2, 2, 56, 128), f32),
             VMEM((NX + 2, 2, 56, 128), f32),
             VMEM((NX, 2, 40, 128), f32),
             VMEM((2, 40, 128), f32),
             VMEM((1024, 384), bf16),
+            VMEM((BASIS + 1, 20, 2, 24, 128), f32),
+            VMEM((20, 2, 24, 128), f32),
+            VMEM((20, 2, 24, 128), f32),
+            pltpu.SemaphoreType.DMA((BASIS + 3,)),
         ],
         compiler_params=pltpu.CompilerParams(vmem_limit_bytes=28 << 20),
         name="basis",
@@ -307,10 +329,17 @@
     return pl.pallas_call(
         finish_kernel,
         out_shape=[jax.ShapeDtypeStruct((4, 8, 128), f32)] * 2,
-        in_specs=[pl.BlockSpec(memory_space=VMEM)] * 4,
+        in_specs=[pl.BlockSpec(memory_space=m) for m in (VMEM, pltpu.HBM, pltpu.HBM, pltpu.HBM)],
         out_specs=[pl.BlockSpec(memory_space=VMEM)] * 2,
-        scratch_shapes=[VMEM((22, 2, 40, 128), f32), VMEM((22, 2, 40, 128), f32)],
-        compiler_params=pltpu.CompilerParams(vmem_limit_bytes=28 << 20),
+        scratch_shapes=[
+            VMEM((22, 2, 40, 128), f32),
+            VMEM((22, 2, 40, 128), f32),
+            VMEM((BASIS + 1, 20, 2, 24, 128), f32),
+            VMEM((20, 2, 24, 128), f32),
+            VMEM((20, 2, 24, 128), f32),
+            pltpu.SemaphoreType.DMA((3,)),
+        ],
+        compiler_params=pltpu.CompilerParams(vmem_limit_bytes=60 << 20),
         name="finish",
         interpret=interpret,
     )(rows, kept, ka, kb)

time: 134 us -> 133 us (level)
  local copies, waits for them, and re-layouts: 7.51 us -> 3.26 us
  Pallas kernels: 16.4 us -> 18.5 us
    unnamed x5 -> x1, local copies, waits for them, and re-layouts: 4.26 us -> 0.01 us
    pallas_call x1, Pallas kernels: 5 us -> 6.71 us  [run_finish(): pl.pallas_call(finish_kernel, out_shape=[jax.ShapeDtypeStruct((4, 8, 128)...]
where the time goes in v4:
time: 133 us; the launch traced here: 132 us
  blocking collectives  49.9 us (38%)
  starting transfers between devices  35.9 us (27%)
  Pallas kernels  18.5 us (14%)
  waiting for transfers between devices  17 us (13%)
  other arithmetic  6.26 us (5%)
  local copies, waits for them, and re-layouts  3.26 us (2%)
    all_to_all x2, blocking collectives, to_all(): lax.all_to_all(jnp.broadcast_to(value[None], (size, *value.shape)), axis,...  36 us
    ppermute x6, starting transfers between devices, shifted(): return lax.ppermute(value, axis_name, pairs)  19.5 us
    all_to_all x1, starting transfers between devices, to_all(): lax.all_to_all(jnp.broadcast_to(value[None], (size, *value.shape)), axis,...  16.4 us
    all_to_all x1, blocking collectives, reduced(): pieces = lax.all_to_all(part, 'gz', 0, 0, tiled=True).sum(axis=0)  14 us
    all_to_all x1, waiting for transfers between devices, to_all(): lax.all_to_all(jnp.broadcast_to(value[None], (size, *value.shape)), axis,...  13.4 us
    pallas_call x1, Pallas kernels, run_basis(): pl.pallas_call(basis_kernel, out_shape=[jax.ShapeDtypeStruct((GZ, 3, SHAR...  11.8 us
    pallas_call x1, Pallas kernels, run_finish(): pl.pallas_call(finish_kernel, out_shape=[jax.ShapeDtypeStruct((4, 8, 128)...  6.71 us
    ppermute x6, waiting for transfers between devices, shifted(): return lax.ppermute(value, axis_name, pairs)  3.64 us
  transfers between devices with their start and end apart: 7, of which 3 were waited for; matrix products, arithmetic and copies ran while one was open for 6% of the time, Pallas kernels for 0%

profile of v4, /device:TPU:1, one launch (start us, length us, event | category | flops | bytes accessed | tf_op | source)
XLA Modules:
  0.0 131.8 jit_solution(4158051446727930018)
XLA Ops:
  0.6 0.9 fusion.10
  1.5 4.1 %collective-permute-start = (f32[2,4,8,16]{3,2,0,1:T(8,128)S(1)}, f32[2,4,8,16]{3,2,0,1:T(8,128)S(1)}, u32[]{:S(2)}, u32[]{:S(2)}) collective-permute-start(f32[2,4,8,16]{3,2,0,1:T(8,128)S(1)} %copy.22), channel_id=1, source_target_pairs={{0,1},{1,2},{2,3},{3,4},{4,5},{5,6},{6,7},{8,9},{9,10},{10,11},{11... | collective-permute-start | bytes 12296 | tf_op jit(solution)/shard_map/ppermute | solution.py:22
  5.6 1.3 collective-permute-start.1
  6.9 0.7 multiply_subtract_fusion
  7.7 0.7 pad_maximum_fusion.1
  8.4 1.9 %collective-permute-done.1 = f32[2,4,8,16]{3,2,1,0:T(8,128)S(1)} collective-permute-done((f32[2,4,8,16]{3,2,1,0:T(8,128)S(1)}, f32[2,4,8,16]{3,2,1,0:T(8,128)S(1)}, u32[]{:S(2)}, u32[]{:S(2)}) %collective-permute-start.1) | collective-permute-done | bytes 4128 | tf_op jit(solution)/shard_map/ppermute | solution.py:22
  10.3 0.1 concatenate.9
  10.4 0.8 broadcast_in_dim.6
  11.2 16.4 %all-to-all-start = ((f32[8,14,8,128]{3,2,1,0:T(8,128)}), f32[8,14,8,128]{3,2,1,0:T(8,128)S(1)}, u32[]{:S(2)}, u32[]{:S(2)}) async-start(f32[8,14,8,128]{3,2,1,0:T(8,128)} %broadcast_in_dim.6), calls=%async_computation | async-start | bytes 917504 | tf_op jit(solution)/shard_map/all_to_all | solution.py:360
  27.7 0.1 pad_add_fusion.at_ref
  27.7 13.4 %all-to-all-done.mid_ref = f32[8,14,8,128]{3,2,1,0:T(8,128)S(1)} async-done(((f32[8,14,8,128]{3,2,1,0:T(8,128)}), f32[8,14,8,128]{3,2,1,0:T(8,128)S(1)}, u32[]{:S(2)}, u32[]{:S(2)}) %all-to-all-start) | async-done | bytes 458784 | tf_op jit(solution)/shard_map/all_to_all | solution.py:360
  41.2 1.3 collective-permute-start.5
  42.5 5.4 %collective-permute-start.4 = (f32[8,10,8,128]{3,2,1,0:T(8,128)S(1)}, f32[8,10,8,128]{3,2,1,0:T(8,128)S(1)}, u32[]{:S(2)}, u32[]{:S(2)}) collective-permute-start(f32[8,10,8,128]{3,2,1,0:T(8,128)S(1)} %slice.56), channel_id=1, source_target_pairs={{8,0},{16,8},{24,16},{32,24},{40,32},{48,40},{56,48},{64,56},{72,6... | collective-permute-start | bytes 983048 | tf_op jit(solution)/shard_map/ppermute | solution.py:22
  47.9 4.2 %collective-permute-start.3 = (f32[8,10,8,128]{3,2,1,0:T(8,128)S(1)}, f32[8,10,8,128]{3,2,1,0:T(8,128)S(1)}, u32[]{:S(2)}, u32[]{:S(2)}) collective-permute-start(f32[8,10,8,128]{3,2,1,0:T(8,128)S(1)} %slice.56), channel_id=1, source_target_pairs={{0,8},{8,16},{16,24},{24,32},{32,40},{40,48},{48,56},{56,64},{64,7... | collective-permute-start | bytes 983048 | tf_op jit(solution)/shard_map/ppermute | solution.py:22
  52.1 3.1 %collective-permute-start.2 = (f32[8,10,8,128]{3,2,1,0:T(8,128)S(1)}, f32[8,10,8,128]{3,2,1,0:T(8,128)S(1)}, u32[]{:S(2)}, u32[]{:S(2)}) collective-permute-start(f32[8,10,8,128]{3,2,1,0:T(8,128)S(1)} %slice.56), channel_id=1, source_target_pairs={{0,16},{8,24},{16,32},{24,40},{32,48},{40,56},{48,64},{56,72},{64,... | collective-permute-start | bytes 983048 | tf_op jit(solution)/shard_map/ppermute | solution.py:22
  55.2 0.8 dynamic_slice.9
  56.0 0.8 dynamic_slice.10
  56.8 0.8 dynamic_slice.11
  57.5 0.6 convert_dynamic-update-slice_fusion.1
  58.1 0.6 convert_dynamic-update-slice_fusion
  58.6 0.6 fusion.7
  59.2 0.6 fusion.8
  59.8 0.6 fusion.6
  60.4 0.6 convert_dynamic-update-slice_fusion.2.table_ref
  61.0 0.2 fusion.14
  61.2 0.1 fusion.19
  61.4 1.7 %collective-permute-done.2.ym2_ref = f32[8,10,8,128]{3,2,1,0:T(8,128)S(1)} collective-permute-done((f32[8,10,8,128]{3,2,1,0:T(8,128)S(1)}, f32[8,10,8,128]{3,2,1,0:T(8,128)S(1)}, u32[]{:S(2)}, u32[]{:S(2)}) %collective-permute-start.2) | collective-permute-done | bytes 327712 | tf_op jit(solution)/shard_map/ppermute | solution.py:22
  63.1 11.8 %basis.1 = (f32[8,3,256]{2,1,0:T(4,128)S(1)}, f32[9,20,2,24,128]{4,3,2,1,0:T(8,128)}, f32[20,2,24,128]{3,2,1,0:T(8,128)}, f32[20,2,24,128]{3,2,1,0:T(8,128)}) custom-call(s32[3]{0:T(128)S(1)} %pad_add_fusion.at_ref, f32[8,14,8,128]{3,2,1,0:T(8,128)S(1)} %all-to-all-done.mid_ref, f32[8,10,8,128]{3,2,1,0:T(8,128)S(1)} %collective-permute-done.2.ym2_ref, ...), custom_call_target="tpu_custom_call" | custom-call | tf_op jit(solution)/shard_map/basis/pallas_call | solution.py:301
  74.9 14.0 %all_to_all.20 = f32[8,3,256]{2,1,0:T(4,128)S(1)} all-to-all(f32[8,3,256]{2,1,0:T(4,128)S(1)} %get-tuple-element.14), channel_id=1, replica_groups=mesh['gx'=8,'gy_0'=8,'gy_1'=2,'gz'=8] {'gz'}, dimensions={0} | all-to-all | bytes 49152 | tf_op jit(solution)/shard_map/all_to_all | solution.py:391
  88.9 17.9 %all_to_all.21 = f32[16,3,256]{2,1,0:T(4,128)S(1)} all-to-all(f32[16,3,256]{2,1,0:T(4,128)S(1)} %broadcast_in_dim.7), channel_id=1, replica_groups=mesh['gx'=8,'gy_0'=8,'gy_1'=2,'gz'=8] {'gy_0','gy_1'}, dimensions={0} | all-to-all | bytes 98304 | tf_op jit(solution)/shard_map/all_to_all | solution.py:360
  106.9 18.1 %all_to_all.22.rows_ref = f32[64,3,256]{2,1,0:T(4,128)} all-to-all(f32[64,3,256]{2,1,0:T(4,128)S(1)} %broadcast_in_dim.8), channel_id=1, replica_groups=mesh['gx'=8,'gy_0'=8,'gy_1'=2,'gz'=8] {'gx','gz'}, dimensions={0} | all-to-all | bytes 393216 | tf_op jit(solution)/shard_map/all_to_all | solution.py:360
  124.9 6.7 %finish.1 = (f32[4,8,128]{2,1,0:T(8,128)}, f32[4,8,128]{2,1,0:T(8,128)}) custom-call(f32[64,3,256]{2,1,0:T(4,128)} %all_to_all.22.rows_ref, f32[9,20,2,24,128]{4,3,2,1,0:T(8,128)} %get-tuple-element.15.far_ref, f32[20,2,24,128]{3,2,1,0:T(8,128)} %get-tuple-element.16.far_a, f32[20,2,24,128]{3,2,1,0:T(8,128)} %get-tuple-element.17.far_b), custom_call_target="tpu_custom_call" | custom-call | tf_op jit(solution)/shard_map/finish/pallas_call | solution.py:329
  (17 shorter events, 0.2 us)
Async XLA Ops:
  1.5 6.9 %collective-permute-start = (f32[2,4,8,16]{3,2,0,1:T(8,128)S(1)}, f32[2,4,8,16]{3,2,0,1:T(8,128)S(1)}, u32[]{:S(2)}, u32[]{:S(2)}) collective-permute-start(f32[2,4,8,16]{3,2,0,1:T(8,128)S(1)} %copy.22), channel_id=1, source_target_pairs={{0,1},{1,2},{2,3},{3,4},{4,5},{5,6},{6,7},{8,9},{9,10},{10,11},{11... | collective-permute-start | bytes 12296 | tf_op jit(solution)/shard_map/ppermute | solution.py:22
  5.6 4.7 %collective-permute-start.1 = (f32[2,4,8,16]{3,2,1,0:T(8,128)S(1)}, f32[2,4,8,16]{3,2,1,0:T(8,128)S(1)}, u32[]{:S(2)}, u32[]{:S(2)}) collective-permute-start(f32[2,4,8,16]{3,2,1,0:T(8,128)S(1)} %get-tuple-element.26), channel_id=1, source_target_pairs={{1,0},{2,1},{3,2},{4,3},{5,4},{6,5},{7,6},{9,8},{10,9},{11,10},{12... | collective-permute-start | bytes 12296 | tf_op jit(solution)/shard_map/ppermute | solution.py:22
  11.2 29.9 %all-to-all-start = ((f32[8,14,8,128]{3,2,1,0:T(8,128)}), f32[8,14,8,128]{3,2,1,0:T(8,128)S(1)}, u32[]{:S(2)}, u32[]{:S(2)}) async-start(f32[8,14,8,128]{3,2,1,0:T(8,128)} %broadcast_in_dim.6), calls=%async_computation | async-start | bytes 917504 | tf_op jit(solution)/shard_map/all_to_all | solution.py:360
  41.2 20.2 %collective-permute-start.5 = (f32[8,10,8,128]{3,2,1,0:T(8,128)S(1)}, f32[8,10,8,128]{3,2,1,0:T(8,128)S(1)}, u32[]{:S(2)}, u32[]{:S(2)}) collective-permute-start(f32[8,10,8,128]{3,2,1,0:T(8,128)S(1)} %slice.56), channel_id=1, source_target_pairs={{16,0},{24,8},{32,16},{40,24},{48,32},{56,40},{64,48},{72,56},{80,... | collective-permute-start | bytes 983048 | tf_op jit(solution)/shard_map/ppermute | solution.py:22
  42.5 18.9 %collective-permute-start.4 = (f32[8,10,8,128]{3,2,1,0:T(8,128)S(1)}, f32[8,10,8,128]{3,2,1,0:T(8,128)S(1)}, u32[]{:S(2)}, u32[]{:S(2)}) collective-permute-start(f32[8,10,8,128]{3,2,1,0:T(8,128)S(1)} %slice.56), channel_id=1, source_target_pairs={{8,0},{16,8},{24,16},{32,24},{40,32},{48,40},{56,48},{64,56},{72,6... | collective-permute-start | bytes 983048 | tf_op jit(solution)/shard_map/ppermute | solution.py:22
  47.9 13.4 %collective-permute-start.3 = (f32[8,10,8,128]{3,2,1,0:T(8,128)S(1)}, f32[8,10,8,128]{3,2,1,0:T(8,128)S(1)}, u32[]{:S(2)}, u32[]{:S(2)}) collective-permute-start(f32[8,10,8,128]{3,2,1,0:T(8,128)S(1)} %slice.56), channel_id=1, source_target_pairs={{0,8},{8,16},{16,24},{24,32},{32,40},{40,48},{48,56},{56,64},{64,7... | collective-permute-start | bytes 983048 | tf_op jit(solution)/shard_map/ppermute | solution.py:22
  52.1 11.0 %collective-permute-start.2 = (f32[8,10,8,128]{3,2,1,0:T(8,128)S(1)}, f32[8,10,8,128]{3,2,1,0:T(8,128)S(1)}, u32[]{:S(2)}, u32[]{:S(2)}) collective-permute-start(f32[8,10,8,128]{3,2,1,0:T(8,128)S(1)} %slice.56), channel_id=1, source_target_pairs={{0,16},{8,24},{16,32},{24,40},{32,48},{40,56},{48,64},{56,72},{64,... | collective-permute-start | bytes 983048 | tf_op jit(solution)/shard_map/ppermute | solution.py:22
